TPU v7x, 512 devices: a whole 4x4x16 slice. The times are simulated.
512 devices in a mesh: dp: 128 (over y_lo, x, z), mp: 4 (over y_hi, core).
Axes of the slice: x: 4, y: 4 (y_hi: 2, y_lo: 2; y = y_hi * 2 + y_lo), z: 16, core: 2. Of those that a mesh axis runs over, the one named last changes fastest.
Arguments:
- vlm_tokens: bfloat16 [32768, 2048], P(('dp', 'mp')), may hold values from -64 to 64
- action_tokens: bfloat16 [65536, 2048], P(('dp', 'mp')), may hold values from -64 to 64
- norm_gain: float32 [2048], replicated, may hold values from 0.25 to 1.75
- proj_old: bfloat16 [4096, 4096], P('dp', 'mp'), may hold values from -0.125 to 0.125
Outputs:
- vlm_hidden: bfloat16 [65536, 4096], P('dp', 'mp')
- action_hidden: bfloat16 [65536, 8192], P('dp', 'mp')
- proj_new: bfloat16 [2048, 8192], P('dp', 'mp')
All inputs are finite; a program needn't handle non-finite values.
Results may differ from a plain program's by a relative error of at most 0.005.
Values may be sent and summed in bfloat16 or wider, within the bound.
No kernel may reach another device: no remote copies, remote signals or barrier semaphores. Data moves between devices by JAX's collectives and lax.ppermute only.
A program may use at most 64 MiB of HBM per device.

v0:
```python
import functools

import jax
import jax.numpy as jnp
from jax import lax
from jax.experimental import pallas as pl
from jax.experimental.pallas import tpu as pltpu
from jax.sharding import Mesh
from jax.sharding import PartitionSpec as P


ALL = ("y", "x", "u", "w", "h", "c")
NX, NU, NW = 4, 4, 4
PLANE = ("x", "u", "w", "c")

epsilon = 1e-06


def normalize(row_values, norm_gain):
    values = row_values.astype(jnp.float32)
    factor = lax.rsqrt(jnp.mean(values * values, axis=-1, keepdims=True) + epsilon)
    return (values * factor * norm_gain).astype(jnp.bfloat16)


def swap(array, axis):
    return lax.ppermute(array, axis, [(0, 1), (1, 0)])


def swap_parity(array):
    return lax.ppermute(array, "w", [(i, i ^ 1) for i in range(NW)])


def along(array, x_core, ahead):
    pairs = []
    for x in range(NX):
        for z in range(NU * NW):
            for c in range(2):
                sx, sz = ((x + ahead) % NX, z) if c == x_core else (x, (z + ahead) % (NU * NW))
                pairs.append(((sx * NU * NW + sz) * 2 + c, (x * NU * NW + z) * 2 + c))
    return lax.ppermute(array, PLANE, pairs)


def both(flag, own, other, dim):
    first = jnp.where(flag == 0, own, other)
    second = jnp.where(flag == 0, other, own)
    return jnp.concatenate([first, second], dim)


def near_weight(proj_old):
    c = lax.axis_index("c")
    half = proj_old.shape[1] // 2
    mine = lax.dynamic_slice_in_dim(proj_old, c * half, half, 1)
    given = lax.dynamic_slice_in_dim(proj_old, (1 - c) * half, half, 1)
    taken = swap(given, "c")
    mates = lax.all_gather(jnp.stack([mine, taken]), "u")
    planes = lax.all_gather(mates, "y")
    after, before = along(planes, 1, 1), along(planes, 1, -1)
    opposite = [along(planes[:1], 1, 2), along(planes[1:], 1, -2)]
    return [planes, after, jnp.concatenate(opposite, 0), before]


def all_weight(pieces):
    part = pieces[0].shape[-1] // 2
    parts = [jnp.stack([p[..., i * part : (i + 1) * part] for p in pieces]) for i in range(2)]
    parts = lax.optimization_barrier(parts)
    near = []
    for i in range(2):
        before = along(parts[i], 0, -1)
        after = along(parts[i], 0, 1)
        near.append((after, before))
    slabs = []
    for i in range(2):
        after, before = near[i]
        half = before.shape[0] // 2
        first = along(before[:half], 0, -1)
        last = along(after[half:], 0, 1)
        slabs.append((parts[i], after, before, first, last))
    return slabs


def chip_tokens(vlm_tokens, action_tokens, norm_gain):
    vlm = normalize(vlm_tokens, norm_gain)
    action = normalize(action_tokens, norm_gain)
    other = swap_parity(vlm)
    pair = both(lax.axis_index("w") % 2, vlm, other, 0)
    return jnp.concatenate([pair, action], 0)


def all_tokens(mine, n_vlm):
    h, c = lax.axis_index("h"), lax.axis_index("c")
    width = mine.shape[1]
    other = swap(mine, "h")
    two = both(h, mine[None], other[None], 0)
    theirs = swap(two, "c")
    four = jnp.stack([jnp.where(c == 0, two, theirs), jnp.where(c == 0, theirs, two)], 1)
    four = four.reshape(4, -1, width)
    normed_vlm = four[:, : 2 * n_vlm].reshape(4, 2, n_vlm, width).transpose(1, 0, 2, 3).reshape(-1, width)
    return normed_vlm, four[:, 2 * n_vlm :].reshape(-1, width)


def new_projection(proj_old):
    b = lax.axis_index("w") % 2
    row_half = proj_old.shape[0] // 2
    kept = lax.dynamic_slice_in_dim(proj_old, b * row_half, row_half, 0)
    given = lax.dynamic_slice_in_dim(proj_old, (1 - b) * row_half, row_half, 0)
    taken = swap_parity(given)
    return both(b, kept, taken, 1)


def gelu(total):
    return total * 0.5 * (1.0 + lax.erf(total * 0.7071067811865476))


ROWS = 256
SLABS = ((0, range(4), 0), (1, range(4), 0), (3, range(4), 0), (2, range(2), 0), (2, range(2, 4), 2))


def weight_copies(place, core, slabs, weight, sems):
    x, w, c = (place[i] for i in range(3))
    part = slabs[0].shape[-1]
    copies = []
    for ref, (r, pieces, start) in zip(slabs, SLABS):
        for q in pieces:
            col = lax.rem(x + jnp.where(c == 0, r, q), NX)
            row = lax.rem(w + jnp.where(c == 0, q, r), NW)
            columns = pl.ds(pl.multiple_of(lax.rem(row, 2) * part, part), part)
            for y in range(2):
                copies.append(
                    pltpu.make_async_copy(
                        ref.at[q - start, y, :, core],
                        weight.at[y, col, :, row // 2, :, columns],
                        sems.at[len(copies)],
                    )
                )
    return copies


def products(place, vlm, action, weight, store):
    depth, part = action.shape[1], weight.shape[-1] // 2
    columns = weight[...].reshape(depth, 2 * part)
    for i in range(0, action.shape[0], ROWS):
        total = jnp.dot(action[i : i + ROWS, :], columns, preferred_element_type=jnp.float32)
        values = gelu(total).astype(jnp.bfloat16)
        store(0, i, values[:, :part])
        store(1, i, values[:, part:])
    columns = weight[..., pl.ds(pl.multiple_of(lax.rem(place[1], 2) * part, part), part)].reshape(depth, part)
    for i in range(0, vlm.shape[0], ROWS):
        total = jnp.dot(vlm[i : i + ROWS, :], columns, preferred_element_type=jnp.float32)
        store(2, i, gelu(total).astype(jnp.bfloat16))


def column_copies(number, core, parts, vlm_out, action_out, sems):
    part = parts.shape[-1]
    starts = [pl.multiple_of((4 * b + 2 * core + number) * part, part) for b in (0, 1, 0)]
    return [
        pltpu.make_async_copy(parts.at[i], out.at[:, pl.ds(starts[i], part)], sems.at[i])
        for i, out in enumerate((action_out, action_out, vlm_out))
    ]


def part_kernel(number, given, own, n_in, place, vlm, action, *refs):
    slabs, refs = refs[: len(SLABS)], list(refs[n_in:])
    given_out = refs.pop(0) if given else None
    vlm_out, action_out = (refs.pop(0), refs.pop(0)) if own else (None, None)
    weights, stage, sems, out_sems = refs
    jobs = [1] * given + [0] * own
    copies = [weight_copies(place, core, slabs, weights.at[n], sems.at[n]) for n, core in enumerate(jobs)]
    for job in copies:
        for copy in job:
            copy.start()
    for n, core in enumerate(jobs):
        for copy in copies[n]:
            copy.wait()
        target = given_out if core else stage
        outs = [] if core else column_copies(number, place[2], stage, vlm_out, action_out, out_sems)

        def store(block, i, values, target=target, outs=outs):
            target[block, i : i + ROWS, :] = values
            if outs and i + ROWS == target.shape[1]:
                outs[block].start()

        products(place, vlm, action, weights.at[n], store)
        for copy in outs:
            copy.wait()


def merge_kernel(place, first, second, vlm_in, action_in, vlm_out, action_out, sems):
    del vlm_in, action_in
    copies = []
    for number, parts in enumerate((first, second)):
        copies += column_copies(number, 1 - place[2], parts, vlm_out, action_out, sems.at[number])
    for copy in copies:
        copy.start()
    for copy in copies:
        copy.wait()


SMEM = pl.BlockSpec(memory_space=pltpu.SMEM)
VMEM = pl.BlockSpec(memory_space=pltpu.VMEM)
HBM = pl.BlockSpec(memory_space=pltpu.HBM)


def outputs(vlm, action, slabs):
    place = jnp.stack([lax.axis_index(a) for a in "xwc"]).astype(jnp.int32)
    part, rows, count, depth = slabs[0][0].shape[-1], slabs[0][0].shape[-2], *action.shape
    taken = jax.ShapeDtypeStruct((3, count, part), jnp.bfloat16)
    wide = tuple(jax.ShapeDtypeStruct((count, n * part), jnp.bfloat16) for n in (4, 8))

    def call(number, given, own, before=()):
        jobs = given + own
        n_in = len(SLABS) + len(before)
        kernel = functools.partial(part_kernel, number, given, own, n_in)
        return pl.pallas_call(
            kernel,
            out_shape=(taken,) * given + wide * own,
            in_specs=[SMEM, VMEM, VMEM] + [HBM] * n_in,
            out_specs=(VMEM,) * given + (HBM, HBM) * own,
            scratch_shapes=[
                pltpu.VMEM((jobs, 2, NX, NU, 2, rows, 2 * part), jnp.bfloat16),
                pltpu.VMEM(taken.shape, taken.dtype),
                pltpu.SemaphoreType.DMA((jobs, 32)),
                pltpu.SemaphoreType.DMA((3,)),
            ],
            input_output_aliases={3 + len(SLABS) + i: given + i for i in range(len(before))},
            compiler_params=pltpu.CompilerParams(vmem_limit_bytes=14 * 1024 * 1024),
            cost_estimate=pl.CostEstimate(
                flops=6 * count * depth * part * jobs, bytes_accessed=6 * 1024 * 1024, transcendentals=0
            ),
        )(place, vlm, action, *slabs[number], *before)

    given_low, *wide_low = call(0, 1, 1)
    taken_low = swap(given_low, "c")
    (given_high,) = call(1, 1, 0)
    taken_high = swap(given_high, "c")
    wide_own = call(1, 0, 1, tuple(wide_low))
    return pl.pallas_call(
        merge_kernel,
        out_shape=wide,
        in_specs=[SMEM, VMEM, VMEM, HBM, HBM],
        out_specs=(HBM, HBM),
        scratch_shapes=[pltpu.SemaphoreType.DMA((2, 3))],
        input_output_aliases={3: 0, 4: 1},
        name="merge",
    )(place, taken_low, taken_high, *wide_own)


def local(vlm_tokens, action_tokens, norm_gain, proj_old):
    pieces = near_weight(proj_old)
    mine = chip_tokens(vlm_tokens, action_tokens, norm_gain)
    slabs = all_weight(pieces)
    vlm, action = all_tokens(mine, vlm_tokens.shape[0])
    vlm_hidden, action_hidden = outputs(vlm, action, slabs)
    return (vlm_hidden, action_hidden, new_projection(proj_old))


def solution(mesh):
    finer = Mesh(mesh.devices.reshape(2, NX, NU, NW, 2, 2), ALL)
    dp, mp = ALL[:4], ALL[4:]
    in_specs = (P(ALL, None), P(ALL, None), P(), P(dp, mp))
    out_specs = (P(dp, mp), P(dp, mp), P(dp, mp))
    return jax.shard_map(local, mesh=finer, in_specs=in_specs, out_specs=out_specs, check_vma=False)
```

profile of v0, /device:TPU:1, one launch (start us, length us, event | category | flops | bytes accessed | tf_op | source)
XLA Modules:
  0.0 159.2 jit_solution(1617052879172881266)
XLA Ops:
  2.9 4.4 %collective-permute-start = (bf16[64,2048]{1,0:T(8,128)(2,1)S(1)}, bf16[64,2048]{1,0:T(8,128)(2,1)S(1)}, u32[]{:S(2)}, u32[]{:S(2)}) collective-permute-start(bf16[64,2048]{1,0:T(8,128)(2,1)S(1)} %fusion.5), channel_id=1, source_target_pairs={{0,4},{4,0},{8,12},{12,8},{1,5},{5,1},{9,13},{13,9},{2,6},{6,2},{1... | collective-permute-start | bytes 786440 | tf_op jit(solution)/shard_map/ppermute | solution.py:30
  11.4 7.0 %collective-permute-start.1 = (bf16[256,2048]{1,0:T(8,128)(2,1)S(1)}, bf16[256,2048]{1,0:T(8,128)(2,1)S(1)}, u32[]{:S(2)}, u32[]{:S(2)}) collective-permute-start(bf16[256,2048]{1,0:T(8,128)(2,1)S(1)} %pad_maximum_fusion.2), channel_id=1, source_target_pairs={{0,2},{2,0},{1,3},{3,1},{4,6},{6,4},{5,7},{7,5},{8,10},{10,8},{9,1... | collective-permute-start | bytes 3145736 | tf_op jit(solution)/shard_map/ppermute | solution.py:26
  18.4 3.8 %collective-permute-start.3 = (bf16[32,512]{1,0:T(8,128)(2,1)S(1)}, bf16[32,512]{1,0:T(8,128)(2,1)S(1)}, u32[]{:S(2)}, u32[]{:S(2)}) collective-permute-start(bf16[32,512]{1,0:T(8,128)(2,1)S(1)} %get-tuple-element.42), channel_id=1, source_target_pairs={{0,1},{1,0},{2,3},{3,2},{4,5},{5,4},{6,7},{7,6},{8,9},{9,8},{10,11... | collective-permute-start | bytes 98312 | tf_op jit(solution)/shard_map/ppermute | solution.py:26
  23.1 24.2 %all-gather = bf16[8,32,512]{2,1,0:T(8,128)(2,1)S(1)} all-gather(bf16[2,32,512]{2,1,0:T(8,128)(2,1)S(1)} %pad_maximum_fusion.5), channel_id=2, replica_groups=mesh['y'=2,'x'=4,'u'=4,'w'=4,'h'=2,'c'=2] {'u'}, dimensions={0}, use_global_device_ids=true | all-gather | bytes 327680 | tf_op jit(solution)/shard_map/all_gather | solution.py:55
  47.3 5.9 %all-gather.1 = bf16[8,2,32,512]{3,2,1,0:T(8,128)(2,1)S(1)} all-gather(bf16[4,2,32,512]{3,2,1,0:T(8,128)(2,1)S(1)} %bitcast.55), channel_id=3, replica_groups=mesh['y'=2,'x'=4,'u'=4,'w'=4,'h'=2,'c'=2] {'y'}, dimensions={0}, use_global_device_ids=true | all-gather | bytes 786432 | tf_op jit(solution)/shard_map/all_gather | solution.py:56
  53.1 4.4 %collective-permute-start.4 = (bf16[2,4,2,32,512]{4,3,2,1,0:T(8,128)(2,1)S(1)}, bf16[2,4,2,32,512]{4,3,2,1,0:T(8,128)(2,1)S(1)}, u32[]{:S(2)}, u32[]{:S(2)}) collective-permute-start(bf16[2,4,2,32,512]{4,3,2,1,0:T(8,128)(2,1)S(1)} %bitcast.52), channel_id=1, source_target_pairs={{4,0},{65,1},{8,4},{69,5},{12,8},{73,9},{16,12},{77,13},{20,16},{8... | collective-permute-start | bytes 1572872 | tf_op jit(solution)/shard_map/ppermute | solution.py:40
  59.5 3.6 %collective-permute-start.5 = (bf16[1,4,2,32,512]{4,3,2,1,0:T(8,128)(2,1)S(1)}, bf16[1,4,2,32,512]{4,3,2,1,0:T(8,128)(2,1)S(1)}, u32[]{:S(2)}, u32[]{:S(2)}) collective-permute-start(bf16[1,4,2,32,512]{4,3,2,1,0:T(8,128)(2,1)S(1)} %get-tuple-element.36), channel_id=1, source_target_pairs={{8,0},{129,1},{12,4},{133,5},{16,8},{137,9},{20,12},{141,13},{24,1... | collective-permute-start | bytes 786440 | tf_op jit(solution)/shard_map/ppermute | solution.py:40
  63.1 3.2 %collective-permute-start.6 = (bf16[1,4,2,32,512]{4,3,2,1,0:T(8,128)(2,1)S(1)}, bf16[1,4,2,32,512]{4,3,2,1,0:T(8,128)(2,1)S(1)}, u32[]{:S(2)}, u32[]{:S(2)}) collective-permute-start(bf16[1,4,2,32,512]{4,3,2,1,0:T(8,128)(2,1)S(1)} %get-tuple-element.35), channel_id=1, source_target_pairs={{56,0},{129,1},{60,4},{133,5},{0,8},{137,9},{4,12},{141,13},{8,16}... | collective-permute-start | bytes 786440 | tf_op jit(solution)/shard_map/ppermute | solution.py:40
  68.9 5.8 %collective-permute-start.2 = (bf16[2,256,2048]{2,1,0:T(8,128)(2,1)}, bf16[2,256,2048]{2,1,0:T(8,128)(2,1)}, u32[]{:S(2)}, u32[]{:S(2)}) collective-permute-start(bf16[2,256,2048]{2,1,0:T(8,128)(2,1)} %pad_maximum_fusion.1), channel_id=1, source_target_pairs={{0,1},{1,0},{2,3},{3,2},{4,5},{5,4},{6,7},{7,6},{8,9},{9,8},{10,11... | collective-permute-start | bytes 6291464 | tf_op jit(solution)/shard_map/ppermute | solution.py:26
  76.1 3.4 %collective-permute-start.9 = (bf16[4,2,4,2,32,256]{5,4,3,2,1,0:T(8,128)(2,1)}, bf16[4,2,4,2,32,256]{5,4,3,2,1,0:T(8,128)(2,1)}, u32[]{:S(2)}, u32[]{:S(2)}) collective-permute-start(bf16[4,2,4,2,32,256]{5,4,3,2,1,0:T(8,128)(2,1)} %get-tuple-element.12.refs_0_), channel_id=1, source_target_pairs={{192,0},{61,1},{196,4},{1,5},{200,8},{5,9},{204,12},{9,13},{208,16... | collective-permute-start | bytes 3145736 | tf_op jit(solution)/shard_map/ppermute | solution.py:40
  79.5 4.6 %collective-permute-start.8 = (bf16[4,2,4,2,32,256]{5,4,3,2,1,0:T(8,128)(2,1)}, bf16[4,2,4,2,32,256]{5,4,3,2,1,0:T(8,128)(2,1)}, u32[]{:S(2)}, u32[]{:S(2)}) collective-permute-start(bf16[4,2,4,2,32,256]{5,4,3,2,1,0:T(8,128)(2,1)} %get-tuple-element.12.refs_0_), channel_id=1, source_target_pairs={{64,0},{5,1},{68,4},{9,5},{72,8},{13,9},{76,12},{17,13},{80,16},{2... | collective-permute-start | bytes 3145736 | tf_op jit(solution)/shard_map/ppermute | solution.py:40
  86.1 4.6 %collective-permute-start.13 = (bf16[4,2,4,2,32,256]{5,4,3,2,1,0:T(8,128)(2,1)S(1)}, bf16[4,2,4,2,32,256]{5,4,3,2,1,0:T(8,128)(2,1)S(1)}, u32[]{:S(2)}, u32[]{:S(2)}) collective-permute-start(bf16[4,2,4,2,32,256]{5,4,3,2,1,0:T(8,128)(2,1)S(1)} %get-tuple-element.14.refs_0_), channel_id=1, source_target_pairs={{64,0},{5,1},{68,4},{9,5},{72,8},{13,9},{76,12},{17,13},{80,16},{2... | collective-permute-start | bytes 3145736 | tf_op jit(solution)/shard_map/ppermute | solution.py:40
  90.7 4.3 %collective-permute-done.9.refs_2_ = bf16[4,2,4,2,32,256]{5,4,3,2,1,0:T(8,128)(2,1)} collective-permute-done((bf16[4,2,4,2,32,256]{5,4,3,2,1,0:T(8,128)(2,1)}, bf16[4,2,4,2,32,256]{5,4,3,2,1,0:T(8,128)(2,1)}, u32[]{:S(2)}, u32[]{:S(2)}) %collective-permute-start.9) | collective-permute-done | bytes 1048608 | tf_op jit(solution)/shard_map/ppermute | solution.py:40
  99.1 4.6 %collective-permute-start.11 = (bf16[2,2,4,2,32,256]{5,4,3,2,1,0:T(8,128)(2,1)S(1)}, bf16[2,2,4,2,32,256]{5,4,3,2,1,0:T(8,128)(2,1)S(1)}, u32[]{:S(2)}, u32[]{:S(2)}) collective-permute-start(bf16[2,2,4,2,32,256]{5,4,3,2,1,0:T(8,128)(2,1)S(1)} %slice.79), channel_id=1, source_target_pairs={{64,0},{5,1},{68,4},{9,5},{72,8},{13,9},{76,12},{17,13},{80,16},{2... | collective-permute-start | bytes 1572872 | tf_op jit(solution)/shard_map/ppermute | solution.py:40
  103.7 2.4 %collective-permute-done.14.refs_2_ = bf16[4,2,4,2,32,256]{5,4,3,2,1,0:T(8,128)(2,1)S(1)} collective-permute-done((bf16[4,2,4,2,32,256]{5,4,3,2,1,0:T(8,128)(2,1)S(1)}, bf16[4,2,4,2,32,256]{5,4,3,2,1,0:T(8,128)(2,1)S(1)}, u32[]{:S(2)}, u32[]{:S(2)}) %collective-permute-start.14) | collective-permute-done | bytes 1048608 | tf_op jit(solution)/shard_map/ppermute | solution.py:40
  108.2 4.6 %collective-permute-start.16 = (bf16[2,2,4,2,32,256]{5,4,3,2,1,0:T(8,128)(2,1)S(1)}, bf16[2,2,4,2,32,256]{5,4,3,2,1,0:T(8,128)(2,1)S(1)}, u32[]{:S(2)}, u32[]{:S(2)}) collective-permute-start(bf16[2,2,4,2,32,256]{5,4,3,2,1,0:T(8,128)(2,1)S(1)} %slice.81), channel_id=1, source_target_pairs={{64,0},{5,1},{68,4},{9,5},{72,8},{13,9},{76,12},{17,13},{80,16},{2... | collective-permute-start | bytes 1572872 | tf_op jit(solution)/shard_map/ppermute | solution.py:40
  112.8 2.1 %select_bitcast_fusion.1 = (bf16[2,1,256,2048]{3,2,1,0:T(8,128)(2,1)S(1)}, bf16[2,1,256,2048]{3,2,1,0:T(8,128)(2,1)S(1)}) fusion(bf16[2,256,2048]{2,1,0:T(8,128)(2,1)} %collective-permute-done.2, pred[]{:T(512)S(6)} %eq.9, bf16[1,256,2048]{2,1,0:T(8,128)(2,1)S(1)} %copy-done.16, bf16[1,256,2048]{2,1,0:T(8,128)(2,1)S(1)} %copy-done.14), kind=kLoop, calls=%fused_computation.3 | loop fusion | flops 3145728 | bytes 8388609 | tf_op jit(solution)/shard_map/stack | solution.py:95
  118.8 4.3 %shard_map.68 = bf16[3,512,256]{2,1,0:T(8,128)(2,1)} custom-call(s32[3]{0:T(128)S(1)} %pad_add_fusion.place, bf16[512,2048]{1,0:T(8,128)(2,1)S(1)} %bitcast.44, bf16[512,2048]{1,0:T(8,128)(2,1)S(1)} %bitcast.47, bf16[4,2,4,2,32,256]{5,4,3,2,1,0:T(8,128)(2,1)S(1)} %get-tuple-element.14.refs_0_, bf16[4,2,4,2,32,256]{5,4,3,2,1,0:T(8,128)(2,1)S(1)} %copy-done.6, ...), custom_call_target="tpu_custom_call" | custom-call | flops 1610612736 | bytes 6291456 | tf_op jit(solution)/shard_map/pallas_call | solution.py:213
  123.2 5.3 %collective-permute-start.17 = (bf16[3,512,256]{2,1,0:T(8,128)(2,1)}, bf16[3,512,256]{2,1,0:T(8,128)(2,1)}, u32[]{:S(2)}, u32[]{:S(2)}) collective-permute-start(bf16[3,512,256]{2,1,0:T(8,128)(2,1)} %shard_map.68), channel_id=1, source_target_pairs={{0,1},{1,0},{2,3},{3,2},{4,5},{5,4},{6,7},{7,6},{8,9},{9,8},{10,11... | collective-permute-start | bytes 2359304 | tf_op jit(solution)/shard_map/ppermute | solution.py:26
  128.5 8.2 %shard_map.67 = (bf16[3,512,256]{2,1,0:T(8,128)(2,1)}, bf16[512,1024]{1,0:T(8,128)(2,1)}, bf16[512,2048]{1,0:T(8,128)(2,1)}) custom-call(s32[3]{0:T(128)S(1)} %pad_add_fusion.place, bf16[512,2048]{1,0:T(8,128)(2,1)S(1)} %bitcast.45, bf16[512,2048]{1,0:T(8,128)(2,1)S(1)} %bitcast.48, bf16[4,2,4,2,32,256]{5,4,3,2,1,0:T(8,128)(2,1)} %get-tuple-element.12.refs_0_, ...), custom_call_target="tpu_custom_call" | custom-call | flops 3221225472 | bytes 6291456 | tf_op jit(solution)/shard_map/pallas_call | solution.py:213
  136.7 1.9 %collective-permute-start.12 = (bf16[3,512,256]{2,1,0:T(8,128)(2,1)}, bf16[3,512,256]{2,1,0:T(8,128)(2,1)}, u32[]{:S(2)}, u32[]{:S(2)}) collective-permute-start(bf16[3,512,256]{2,1,0:T(8,128)(2,1)} %get-tuple-element.13), channel_id=1, source_target_pairs={{0,1},{1,0},{2,3},{3,2},{4,5},{5,4},{6,7},{7,6},{8,9},{9,8},{10,11... | collective-permute-start | bytes 2359304 | tf_op jit(solution)/shard_map/ppermute | solution.py:26
  138.7 5.8 %collective-permute-start.18 = (bf16[16,1024]{1,0:T(8,128)(2,1)S(1)}, bf16[16,1024]{1,0:T(8,128)(2,1)S(1)}, u32[]{:S(2)}, u32[]{:S(2)}) collective-permute-start(bf16[16,1024]{1,0:T(8,128)(2,1)S(1)} %constant_dynamic-slice_fusion), channel_id=1, source_target_pairs={{0,4},{4,0},{8,12},{12,8},{1,5},{5,1},{9,13},{13,9},{2,6},{6,2},{1... | collective-permute-start | bytes 98312 | tf_op jit(solution)/shard_map/ppermute | solution.py:30
  152.6 4.0 %shard_map.69 = (bf16[512,1024]{1,0:T(8,128)(2,1)}, bf16[512,2048]{1,0:T(8,128)(2,1)}) custom-call(s32[3]{0:T(128)S(1)} %pad_add_fusion.place, bf16[512,2048]{1,0:T(8,128)(2,1)S(1)} %bitcast.46, bf16[512,2048]{1,0:T(8,128)(2,1)S(1)} %bitcast.49, ...), custom_call_target="tpu_custom_call", output_to_operand_aliasing={{0}: (8, {}), {1}: (9, {})} | custom-call | flops 1610612736 | bytes 6291456 | tf_op jit(solution)/shard_map/pallas_call | solution.py:213
  156.6 2.6 %merge.1 = (bf16[512,1024]{1,0:T(8,128)(2,1)}, bf16[512,2048]{1,0:T(8,128)(2,1)}) custom-call(s32[3]{0:T(128)} %copy-done.12, bf16[3,512,256]{2,1,0:T(8,128)(2,1)} %collective-permute-done.12.first, bf16[3,512,256]{2,1,0:T(8,128)(2,1)} %collective-permute-done.17.second, ...), custom_call_target="tpu_custom_call", output_to_operand_aliasing={{0}: (3, {}), {1}: (4, {})} | custom-call | tf_op jit(solution)/shard_map/merge/pallas_call | solution.py:236
  (92 shorter events, 33.1 us)
Async XLA Ops:
  0.6 10.4 %copy-start.17 = (bf16[64,2048]{1,0:T(8,128)(2,1)S(1)}, bf16[64,2048]{1,0:T(8,128)(2,1)}, u32[]{:S(2)}) copy-start(bf16[64,2048]{1,0:T(8,128)(2,1)} %param.4) | copy-start | bytes 786436
  2.9 8.1 %collective-permute-start = (bf16[64,2048]{1,0:T(8,128)(2,1)S(1)}, bf16[64,2048]{1,0:T(8,128)(2,1)S(1)}, u32[]{:S(2)}, u32[]{:S(2)}) collective-permute-start(bf16[64,2048]{1,0:T(8,128)(2,1)S(1)} %fusion.5), channel_id=1, source_target_pairs={{0,4},{4,0},{8,12},{12,8},{1,5},{5,1},{9,13},{13,9},{2,6},{6,2},{1... | collective-permute-start | bytes 786440 | tf_op jit(solution)/shard_map/ppermute | solution.py:30
  11.4 55.0 %collective-permute-start.1 = (bf16[256,2048]{1,0:T(8,128)(2,1)S(1)}, bf16[256,2048]{1,0:T(8,128)(2,1)S(1)}, u32[]{:S(2)}, u32[]{:S(2)}) collective-permute-start(bf16[256,2048]{1,0:T(8,128)(2,1)S(1)} %pad_maximum_fusion.2), channel_id=1, source_target_pairs={{0,2},{2,0},{1,3},{3,1},{4,6},{6,4},{5,7},{7,5},{8,10},{10,8},{9,1... | collective-permute-start | bytes 3145736 | tf_op jit(solution)/shard_map/ppermute | solution.py:26
  18.4 4.7 %collective-permute-start.3 = (bf16[32,512]{1,0:T(8,128)(2,1)S(1)}, bf16[32,512]{1,0:T(8,128)(2,1)S(1)}, u32[]{:S(2)}, u32[]{:S(2)}) collective-permute-start(bf16[32,512]{1,0:T(8,128)(2,1)S(1)} %get-tuple-element.42), channel_id=1, source_target_pairs={{0,1},{1,0},{2,3},{3,2},{4,5},{5,4},{6,7},{7,6},{8,9},{9,8},{10,11... | collective-permute-start | bytes 98312 | tf_op jit(solution)/shard_map/ppermute | solution.py:26
  53.1 21.6 %collective-permute-start.4 = (bf16[2,4,2,32,512]{4,3,2,1,0:T(8,128)(2,1)S(1)}, bf16[2,4,2,32,512]{4,3,2,1,0:T(8,128)(2,1)S(1)}, u32[]{:S(2)}, u32[]{:S(2)}) collective-permute-start(bf16[2,4,2,32,512]{4,3,2,1,0:T(8,128)(2,1)S(1)} %bitcast.52), channel_id=1, source_target_pairs={{4,0},{65,1},{8,4},{69,5},{12,8},{73,9},{16,12},{77,13},{20,16},{8... | collective-permute-start | bytes 1572872 | tf_op jit(solution)/shard_map/ppermute | solution.py:40
  57.5 17.3 %collective-permute-start.7 = (bf16[2,4,2,32,512]{4,3,2,1,0:T(8,128)(2,1)S(1)}, bf16[2,4,2,32,512]{4,3,2,1,0:T(8,128)(2,1)S(1)}, u32[]{:S(2)}, u32[]{:S(2)}) collective-permute-start(bf16[2,4,2,32,512]{4,3,2,1,0:T(8,128)(2,1)S(1)} %bitcast.53), channel_id=1, source_target_pairs={{60,0},{193,1},{0,4},{197,5},{4,8},{201,9},{8,12},{205,13},{12,16}... | collective-permute-start | bytes 1572872 | tf_op jit(solution)/shard_map/ppermute | solution.py:40
  59.5 15.1 %collective-permute-start.5 = (bf16[1,4,2,32,512]{4,3,2,1,0:T(8,128)(2,1)S(1)}, bf16[1,4,2,32,512]{4,3,2,1,0:T(8,128)(2,1)S(1)}, u32[]{:S(2)}, u32[]{:S(2)}) collective-permute-start(bf16[1,4,2,32,512]{4,3,2,1,0:T(8,128)(2,1)S(1)} %get-tuple-element.36), channel_id=1, source_target_pairs={{8,0},{129,1},{12,4},{133,5},{16,8},{137,9},{20,12},{141,13},{24,1... | collective-permute-start | bytes 786440 | tf_op jit(solution)/shard_map/ppermute | solution.py:40
  63.1 11.5 %collective-permute-start.6 = (bf16[1,4,2,32,512]{4,3,2,1,0:T(8,128)(2,1)S(1)}, bf16[1,4,2,32,512]{4,3,2,1,0:T(8,128)(2,1)S(1)}, u32[]{:S(2)}, u32[]{:S(2)}) collective-permute-start(bf16[1,4,2,32,512]{4,3,2,1,0:T(8,128)(2,1)S(1)} %get-tuple-element.35), channel_id=1, source_target_pairs={{56,0},{129,1},{60,4},{133,5},{0,8},{137,9},{4,12},{141,13},{8,16}... | collective-permute-start | bytes 786440 | tf_op jit(solution)/shard_map/ppermute | solution.py:40
  68.9 43.9 %collective-permute-start.2 = (bf16[2,256,2048]{2,1,0:T(8,128)(2,1)}, bf16[2,256,2048]{2,1,0:T(8,128)(2,1)}, u32[]{:S(2)}, u32[]{:S(2)}) collective-permute-start(bf16[2,256,2048]{2,1,0:T(8,128)(2,1)} %pad_maximum_fusion.1), channel_id=1, source_target_pairs={{0,1},{1,0},{2,3},{3,2},{4,5},{5,4},{6,7},{7,6},{8,9},{9,8},{10,11... | collective-permute-start | bytes 6291464 | tf_op jit(solution)/shard_map/ppermute | solution.py:26
  76.1 18.8 %collective-permute-start.9 = (bf16[4,2,4,2,32,256]{5,4,3,2,1,0:T(8,128)(2,1)}, bf16[4,2,4,2,32,256]{5,4,3,2,1,0:T(8,128)(2,1)}, u32[]{:S(2)}, u32[]{:S(2)}) collective-permute-start(bf16[4,2,4,2,32,256]{5,4,3,2,1,0:T(8,128)(2,1)} %get-tuple-element.12.refs_0_), channel_id=1, source_target_pairs={{192,0},{61,1},{196,4},{1,5},{200,8},{5,9},{204,12},{9,13},{208,16... | collective-permute-start | bytes 3145736 | tf_op jit(solution)/shard_map/ppermute | solution.py:40
  79.5 18.5 %collective-permute-start.8 = (bf16[4,2,4,2,32,256]{5,4,3,2,1,0:T(8,128)(2,1)}, bf16[4,2,4,2,32,256]{5,4,3,2,1,0:T(8,128)(2,1)}, u32[]{:S(2)}, u32[]{:S(2)}) collective-permute-start(bf16[4,2,4,2,32,256]{5,4,3,2,1,0:T(8,128)(2,1)} %get-tuple-element.12.refs_0_), channel_id=1, source_target_pairs={{64,0},{5,1},{68,4},{9,5},{72,8},{13,9},{76,12},{17,13},{80,16},{2... | collective-permute-start | bytes 3145736 | tf_op jit(solution)/shard_map/ppermute | solution.py:40
  84.1 22.0 %collective-permute-start.14 = (bf16[4,2,4,2,32,256]{5,4,3,2,1,0:T(8,128)(2,1)S(1)}, bf16[4,2,4,2,32,256]{5,4,3,2,1,0:T(8,128)(2,1)S(1)}, u32[]{:S(2)}, u32[]{:S(2)}) collective-permute-start(bf16[4,2,4,2,32,256]{5,4,3,2,1,0:T(8,128)(2,1)S(1)} %get-tuple-element.14.refs_0_), channel_id=1, source_target_pairs={{192,0},{61,1},{196,4},{1,5},{200,8},{5,9},{204,12},{9,13},{208,16... | collective-permute-start | bytes 3145736 | tf_op jit(solution)/shard_map/ppermute | solution.py:40
  86.1 22.0 %collective-permute-start.13 = (bf16[4,2,4,2,32,256]{5,4,3,2,1,0:T(8,128)(2,1)S(1)}, bf16[4,2,4,2,32,256]{5,4,3,2,1,0:T(8,128)(2,1)S(1)}, u32[]{:S(2)}, u32[]{:S(2)}) collective-permute-start(bf16[4,2,4,2,32,256]{5,4,3,2,1,0:T(8,128)(2,1)S(1)} %get-tuple-element.14.refs_0_), channel_id=1, source_target_pairs={{64,0},{5,1},{68,4},{9,5},{72,8},{13,9},{76,12},{17,13},{80,16},{2... | collective-permute-start | bytes 3145736 | tf_op jit(solution)/shard_map/ppermute | solution.py:40
  90.7 55.7 %copy-start.12 = (s32[3]{0:T(128)}, s32[3]{0:T(128)S(1)}, u32[]{:S(2)}) copy-start(s32[3]{0:T(128)S(1)} %pad_add_fusion.place) | copy-start | bytes 40
  90.7 22.0 %copy-start.14 = (bf16[1,256,2048]{2,1,0:T(8,128)(2,1)S(1)}, bf16[1,256,2048]{2,1,0:T(8,128)(2,1)}, u32[]{:S(2)}) copy-start(bf16[1,256,2048]{2,1,0:T(8,128)(2,1)} %copy-done.13) | copy-start | bytes 3145732
  90.7 22.0 %copy-start.16 = (bf16[1,256,2048]{2,1,0:T(8,128)(2,1)S(1)}, bf16[1,256,2048]{2,1,0:T(8,128)(2,1)}, u32[]{:S(2)}) copy-start(bf16[1,256,2048]{2,1,0:T(8,128)(2,1)} %copy-done.15) | copy-start | bytes 3145732
  96.1 32.4 %collective-permute-start.10 = (bf16[2,2,4,2,32,256]{5,4,3,2,1,0:T(8,128)(2,1)S(1)}, bf16[2,2,4,2,32,256]{5,4,3,2,1,0:T(8,128)(2,1)S(1)}, u32[]{:S(2)}, u32[]{:S(2)}) collective-permute-start(bf16[2,2,4,2,32,256]{5,4,3,2,1,0:T(8,128)(2,1)S(1)} %slice.78), channel_id=1, source_target_pairs={{192,0},{61,1},{196,4},{1,5},{200,8},{5,9},{204,12},{9,13},{208,16... | collective-permute-start | bytes 1572872 | tf_op jit(solution)/shard_map/ppermute | solution.py:40
  99.1 29.4 %collective-permute-start.11 = (bf16[2,2,4,2,32,256]{5,4,3,2,1,0:T(8,128)(2,1)S(1)}, bf16[2,2,4,2,32,256]{5,4,3,2,1,0:T(8,128)(2,1)S(1)}, u32[]{:S(2)}, u32[]{:S(2)}) collective-permute-start(bf16[2,2,4,2,32,256]{5,4,3,2,1,0:T(8,128)(2,1)S(1)} %slice.79), channel_id=1, source_target_pairs={{64,0},{5,1},{68,4},{9,5},{72,8},{13,9},{76,12},{17,13},{80,16},{2... | collective-permute-start | bytes 1572872 | tf_op jit(solution)/shard_map/ppermute | solution.py:40
  106.2 11.4 %collective-permute-start.15 = (bf16[2,2,4,2,32,256]{5,4,3,2,1,0:T(8,128)(2,1)S(1)}, bf16[2,2,4,2,32,256]{5,4,3,2,1,0:T(8,128)(2,1)S(1)}, u32[]{:S(2)}, u32[]{:S(2)}) collective-permute-start(bf16[2,2,4,2,32,256]{5,4,3,2,1,0:T(8,128)(2,1)S(1)} %slice.80), channel_id=1, source_target_pairs={{192,0},{61,1},{196,4},{1,5},{200,8},{5,9},{204,12},{9,13},{208,16... | collective-permute-start | bytes 1572872 | tf_op jit(solution)/shard_map/ppermute | solution.py:40
  108.2 10.7 %collective-permute-start.16 = (bf16[2,2,4,2,32,256]{5,4,3,2,1,0:T(8,128)(2,1)S(1)}, bf16[2,2,4,2,32,256]{5,4,3,2,1,0:T(8,128)(2,1)S(1)}, u32[]{:S(2)}, u32[]{:S(2)}) collective-permute-start(bf16[2,2,4,2,32,256]{5,4,3,2,1,0:T(8,128)(2,1)S(1)} %slice.81), channel_id=1, source_target_pairs={{64,0},{5,1},{68,4},{9,5},{72,8},{13,9},{76,12},{17,13},{80,16},{2... | collective-permute-start | bytes 1572872 | tf_op jit(solution)/shard_map/ppermute | solution.py:40
  115.9 12.7 %copy-start = (bf16[4,128,2048]{2,1,0:T(8,128)(2,1)}, bf16[4,128,2048]{2,1,0:T(8,128)(2,1)S(1)}, u32[]{:S(2)}) copy-start(bf16[4,128,2048]{2,1,0:T(8,128)(2,1)S(1)} %get-tuple-element.21) | copy-start | bytes 6291460
  123.2 33.4 %collective-permute-start.17 = (bf16[3,512,256]{2,1,0:T(8,128)(2,1)}, bf16[3,512,256]{2,1,0:T(8,128)(2,1)}, u32[]{:S(2)}, u32[]{:S(2)}) collective-permute-start(bf16[3,512,256]{2,1,0:T(8,128)(2,1)} %shard_map.68), channel_id=1, source_target_pairs={{0,1},{1,0},{2,3},{3,2},{4,5},{5,4},{6,7},{7,6},{8,9},{9,8},{10,11... | collective-permute-start | bytes 2359304 | tf_op jit(solution)/shard_map/ppermute | solution.py:26
  136.7 19.9 %collective-permute-start.12 = (bf16[3,512,256]{2,1,0:T(8,128)(2,1)}, bf16[3,512,256]{2,1,0:T(8,128)(2,1)}, u32[]{:S(2)}, u32[]{:S(2)}) collective-permute-start(bf16[3,512,256]{2,1,0:T(8,128)(2,1)} %get-tuple-element.13), channel_id=1, source_target_pairs={{0,1},{1,0},{2,3},{3,2},{4,5},{5,4},{6,7},{7,6},{8,9},{9,8},{10,11... | collective-permute-start | bytes 2359304 | tf_op jit(solution)/shard_map/ppermute | solution.py:26
  138.7 7.1 %collective-permute-start.18 = (bf16[16,1024]{1,0:T(8,128)(2,1)S(1)}, bf16[16,1024]{1,0:T(8,128)(2,1)S(1)}, u32[]{:S(2)}, u32[]{:S(2)}) collective-permute-start(bf16[16,1024]{1,0:T(8,128)(2,1)S(1)} %constant_dynamic-slice_fusion), channel_id=1, source_target_pairs={{0,4},{4,0},{8,12},{12,8},{1,5},{5,1},{9,13},{13,9},{2,6},{6,2},{1... | collective-permute-start | bytes 98312 | tf_op jit(solution)/shard_map/ppermute | solution.py:30
  (15 other events, 61.5 us)
where the time goes:
time: 161 us; the launch traced here: 159 us
  starting transfers between devices  74.5 us (46%)
  blocking collectives  30.1 us (19%)
  Pallas kernels  19.1 us (12%)
  waiting for transfers between devices  12.9 us (8%)
  other arithmetic  11.7 us (7%)
  local copies, waits for them, and re-layouts  9.67 us (6%)
    ppermute x12, starting transfers between devices, along(): return lax.ppermute(array, PLANE, pairs)  40.5 us
    all_gather x1, blocking collectives, near_weight(): mates = lax.all_gather(jnp.stack([mine, taken]), 'u')  24.2 us
    ppermute x5, starting transfers between devices, swap(): return lax.ppermute(array, axis, [(0, 1), (1, 0)])  23.8 us
    pallas_call x3, Pallas kernels, call(): pl.pallas_call(kernel, out_shape=(taken,) * given + wide * own, in_specs=...  16.5 us
    ppermute x2, starting transfers between devices, swap_parity(): return lax.ppermute(array, 'w', [(i, i ^ 1) for i in range(NW)])  10.2 us
    ppermute x12, waiting for transfers between devices, along(): return lax.ppermute(array, PLANE, pairs)  9.53 us
    unnamed x41, local copies, waits for them, and re-layouts  6.49 us
    all_gather x1, blocking collectives, near_weight(): planes = lax.all_gather(mates, 'y')  5.87 us
  transfers between devices with their start and end apart: 19, of which 7 were waited for; matrix products, arithmetic and copies ran while one was open for 8% of the time, Pallas kernels for 10%

commit v1 on v0

--- a/solution.py
+++ b/solution.py
@@ -61,29 +61,31 @@
 
 def all_weight(pieces):
     part = pieces[0].shape[-1] // 2
-    parts = [jnp.stack([p[..., i * part : (i + 1) * part] for p in pieces]) for i in range(2)]
-    parts = lax.optimization_barrier(parts)
-    near = []
-    for i in range(2):
-        before = along(parts[i], 0, -1)
-        after = along(parts[i], 0, 1)
-        near.append((after, before))
-    slabs = []
-    for i in range(2):
-        after, before = near[i]
-        half = before.shape[0] // 2
-        first = along(before[:half], 0, -1)
-        last = along(after[half:], 0, 1)
-        slabs.append((parts[i], after, before, first, last))
-    return slabs
-
-
-def chip_tokens(vlm_tokens, action_tokens, norm_gain):
+    low, high = (jnp.stack([p[..., i * part : (i + 1) * part] for p in pieces]) for i in range(2))
+    low, high = lax.optimization_barrier((low, high))
+    low_before = along(low, 0, -1)
+    low_after = along(low, 0, 1)
+    high_before = along(high, 0, -1)
+    high_after = along(high, 0, 1)
+    low_far = along(low_before, 0, -1)
+    high_far = along(high_after, 0, 1)
+    return (low, low_after, low_far, low_before), (high, high_after, high_far, high_before)
+
+
+def pair_exchange(vlm_tokens, action_tokens, norm_gain, proj_old):
+    b = lax.axis_index("w") % 2
+    row_half, width = proj_old.shape[0] // 2, vlm_tokens.shape[1]
     vlm = normalize(vlm_tokens, norm_gain)
     action = normalize(action_tokens, norm_gain)
-    other = swap_parity(vlm)
-    pair = both(lax.axis_index("w") % 2, vlm, other, 0)
-    return jnp.concatenate([pair, action], 0)
+    kept = lax.dynamic_slice_in_dim(proj_old, b * row_half, row_half, 0)
+    given = lax.dynamic_slice_in_dim(proj_old, (1 - b) * row_half, row_half, 0)
+    folds = width // given.shape[1]
+    given = jnp.concatenate(jnp.split(given, folds, 0), 1)
+    other = swap_parity(jnp.concatenate([vlm, given], 0))
+    pair = both(b, vlm, other[: vlm.shape[0]], 0)
+    taken = jnp.concatenate(jnp.split(other[vlm.shape[0] :], folds, 1), 0)
+    rows = both(b, kept, taken, 1)
+    return jnp.concatenate([pair, action], 0), rows
 
 
 def all_tokens(mine, n_vlm):
@@ -98,36 +100,26 @@
     return normed_vlm, four[:, 2 * n_vlm :].reshape(-1, width)
 
 
-def new_projection(proj_old):
-    b = lax.axis_index("w") % 2
-    row_half = proj_old.shape[0] // 2
-    kept = lax.dynamic_slice_in_dim(proj_old, b * row_half, row_half, 0)
-    given = lax.dynamic_slice_in_dim(proj_old, (1 - b) * row_half, row_half, 0)
-    taken = swap_parity(given)
-    return both(b, kept, taken, 1)
-
-
 def gelu(total):
     return total * 0.5 * (1.0 + lax.erf(total * 0.7071067811865476))
 
 
 ROWS = 256
-SLABS = ((0, range(4), 0), (1, range(4), 0), (3, range(4), 0), (2, range(2), 0), (2, range(2, 4), 2))
 
 
 def weight_copies(place, core, slabs, weight, sems):
     x, w, c = (place[i] for i in range(3))
     part = slabs[0].shape[-1]
     copies = []
-    for ref, (r, pieces, start) in zip(slabs, SLABS):
-        for q in pieces:
+    for r, ref in enumerate(slabs):
+        for q in range(4):
             col = lax.rem(x + jnp.where(c == 0, r, q), NX)
             row = lax.rem(w + jnp.where(c == 0, q, r), NW)
             columns = pl.ds(pl.multiple_of(lax.rem(row, 2) * part, part), part)
             for y in range(2):
                 copies.append(
                     pltpu.make_async_copy(
-                        ref.at[q - start, y, :, core],
+                        ref.at[q, y, :, core],
                         weight.at[y, col, :, row // 2, :, columns],
                         sems.at[len(copies)],
                     )
@@ -159,7 +151,7 @@
 
 
 def part_kernel(number, given, own, n_in, place, vlm, action, *refs):
-    slabs, refs = refs[: len(SLABS)], list(refs[n_in:])
+    slabs, refs = refs[:4], list(refs[n_in:])
     given_out = refs.pop(0) if given else None
     vlm_out, action_out = (refs.pop(0), refs.pop(0)) if own else (None, None)
     weights, stage, sems, out_sems = refs
@@ -208,7 +200,7 @@
 
     def call(number, given, own, before=()):
         jobs = given + own
-        n_in = len(SLABS) + len(before)
+        n_in = 4 + len(before)
         kernel = functools.partial(part_kernel, number, given, own, n_in)
         return pl.pallas_call(
             kernel,
@@ -221,7 +213,7 @@
                 pltpu.SemaphoreType.DMA((jobs, 32)),
                 pltpu.SemaphoreType.DMA((3,)),
             ],
-            input_output_aliases={3 + len(SLABS) + i: given + i for i in range(len(before))},
+            input_output_aliases={7 + i: given + i for i in range(len(before))},
             compiler_params=pltpu.CompilerParams(vmem_limit_bytes=14 * 1024 * 1024),
             cost_estimate=pl.CostEstimate(
                 flops=6 * count * depth * part * jobs, bytes_accessed=6 * 1024 * 1024, transcendentals=0
@@ -246,11 +238,11 @@
 
 def local(vlm_tokens, action_tokens, norm_gain, proj_old):
     pieces = near_weight(proj_old)
-    mine = chip_tokens(vlm_tokens, action_tokens, norm_gain)
+    mine, proj_new = pair_exchange(vlm_tokens, action_tokens, norm_gain, proj_old)
     slabs = all_weight(pieces)
     vlm, action = all_tokens(mine, vlm_tokens.shape[0])
     vlm_hidden, action_hidden = outputs(vlm, action, slabs)
-    return (vlm_hidden, action_hidden, new_projection(proj_old))
+    return (vlm_hidden, action_hidden, proj_new)
 
 
 def solution(mesh):

time: 161 us -> 155 us (0.963)
  starting transfers between devices: 74.5 us -> 60 us
  waiting for transfers between devices: 12.9 us -> 22.2 us
  local copies, waits for them, and re-layouts: 9.67 us -> 5.82 us
    ppermute x12 -> x10, waiting for transfers between devices: 9.53 us -> 19.5 us  [along(): return lax.ppermute(array, PLANE, pairs)]
    ppermute x12 -> x10, starting transfers between devices: 40.5 us -> 32.8 us  [along(): return lax.ppermute(array, PLANE, pairs)]
    ppermute x2 -> x1, starting transfers between devices: 10.2 us -> 4.36 us  [swap_parity(): return lax.ppermute(array, 'w', [(i, i ^ 1) for i in range(NW)])]
    unnamed x41 -> x23, local copies, waits for them, and re-layouts: 6.49 us -> 4.1 us
    slice x4 -> x0, local copies, waits for them, and re-layouts: 2.22 us -> none  [the longest x2 1.11 us: all_weight(): last = along(after[half:], 0, 1)]
  transfers between devices with their start and end apart: 19 -> 16, of which waited for: 7 -> 5; matrix products, arithmetic and copies ran while one was open for 8% -> 7% of each run, Pallas kernels for 10% -> 12%
where the time goes in v1:
time: 155 us; the launch traced here: 152 us
  starting transfers between devices  60 us (39%)
  blocking collectives  30.4 us (20%)
  waiting for transfers between devices  22.2 us (14%)
  Pallas kernels  20.6 us (13%)
  other arithmetic  12.2 us (8%)
  local copies, waits for them, and re-layouts  5.82 us (4%)
    ppermute x10, starting transfers between devices, along(): return lax.ppermute(array, PLANE, pairs)  32.8 us
    all_gather x1, blocking collectives, near_weight(): mates = lax.all_gather(jnp.stack([mine, taken]), 'u')  24.5 us
    ppermute x5, starting transfers between devices, swap(): return lax.ppermute(array, axis, [(0, 1), (1, 0)])  22.8 us
    ppermute x10, waiting for transfers between devices, along(): return lax.ppermute(array, PLANE, pairs)  19.5 us
    pallas_call x3, Pallas kernels, call(): pl.pallas_call(kernel, out_shape=(taken,) * given + wide * own, in_specs=...  18 us
    all_gather x1, blocking collectives, near_weight(): planes = lax.all_gather(mates, 'y')  5.87 us
    ppermute x1, starting transfers between devices, swap_parity(): return lax.ppermute(array, 'w', [(i, i ^ 1) for i in range(NW)])  4.36 us
    unnamed x23, local copies, waits for them, and re-layouts  4.1 us
  transfers between devices with their start and end apart: 16, of which 5 were waited for; matrix products, arithmetic and copies ran while one was open for 7% of the time, Pallas kernels for 12%

profile of v1, /device:TPU:1, one launch (start us, length us, event | category | flops | bytes accessed | tf_op | source)
XLA Modules:
  0.0 152.4 jit_solution(2465534144538997484)
XLA Ops:
  3.7 4.4 %collective-permute-start = (bf16[72,2048]{1,0:T(8,128)(2,1)S(1)}, bf16[72,2048]{1,0:T(8,128)(2,1)S(1)}, u32[]{:S(2)}, u32[]{:S(2)}) collective-permute-start(bf16[72,2048]{1,0:T(8,128)(2,1)S(1)} %maximum_maximum_fusion), channel_id=1, source_target_pairs={{0,4},{4,0},{8,12},{12,8},{1,5},{5,1},{9,13},{13,9},{2,6},{6,2},{1... | collective-permute-start | bytes 884744 | tf_op jit(solution)/shard_map/ppermute | solution.py:30
  10.3 1.9 %collective-permute-done = bf16[72,2048]{1,0:T(8,128)(2,1)S(1)} collective-permute-done((bf16[72,2048]{1,0:T(8,128)(2,1)S(1)}, bf16[72,2048]{1,0:T(8,128)(2,1)S(1)}, u32[]{:S(2)}, u32[]{:S(2)}) %collective-permute-start) | collective-permute-done | bytes 294944 | tf_op jit(solution)/shard_map/ppermute | solution.py:30
  12.5 7.3 %collective-permute-start.1 = (bf16[256,2048]{1,0:T(8,128)(2,1)S(1)}, bf16[256,2048]{1,0:T(8,128)(2,1)}, u32[]{:S(2)}, u32[]{:S(2)}) collective-permute-start(bf16[256,2048]{1,0:T(8,128)(2,1)S(1)} %pad_maximum_fusion.2), channel_id=1, source_target_pairs={{0,2},{2,0},{1,3},{3,1},{4,6},{6,4},{5,7},{7,5},{8,10},{10,8},{9,1... | collective-permute-start | bytes 3145736 | tf_op jit(solution)/shard_map/ppermute | solution.py:26
  19.9 3.5 %collective-permute-start.3 = (bf16[32,512]{1,0:T(8,128)(2,1)S(1)}, bf16[32,512]{1,0:T(8,128)(2,1)S(1)}, u32[]{:S(2)}, u32[]{:S(2)}) collective-permute-start(bf16[32,512]{1,0:T(8,128)(2,1)S(1)} %get-tuple-element.44), channel_id=1, source_target_pairs={{0,1},{1,0},{2,3},{3,2},{4,5},{5,4},{6,7},{7,6},{8,9},{9,8},{10,11... | collective-permute-start | bytes 98312 | tf_op jit(solution)/shard_map/ppermute | solution.py:26
  24.3 24.5 %all-gather = bf16[8,32,512]{2,1,0:T(8,128)(2,1)S(1)} all-gather(bf16[2,32,512]{2,1,0:T(8,128)(2,1)S(1)} %pad_maximum_fusion.5), channel_id=2, replica_groups=mesh['y'=2,'x'=4,'u'=4,'w'=4,'h'=2,'c'=2] {'u'}, dimensions={0}, use_global_device_ids=true | all-gather | bytes 327680 | tf_op jit(solution)/shard_map/all_gather | solution.py:55
  48.8 5.9 %all-gather.1 = bf16[8,2,32,512]{3,2,1,0:T(8,128)(2,1)S(1)} all-gather(bf16[4,2,32,512]{3,2,1,0:T(8,128)(2,1)S(1)} %bitcast.55), channel_id=3, replica_groups=mesh['y'=2,'x'=4,'u'=4,'w'=4,'h'=2,'c'=2] {'y'}, dimensions={0}, use_global_device_ids=true | all-gather | bytes 786432 | tf_op jit(solution)/shard_map/all_gather | solution.py:56
  54.7 4.4 %collective-permute-start.4 = (bf16[2,4,2,32,512]{4,3,2,1,0:T(8,128)(2,1)S(1)}, bf16[2,4,2,32,512]{4,3,2,1,0:T(8,128)(2,1)S(1)}, u32[]{:S(2)}, u32[]{:S(2)}) collective-permute-start(bf16[2,4,2,32,512]{4,3,2,1,0:T(8,128)(2,1)S(1)} %bitcast.52), channel_id=1, source_target_pairs={{4,0},{65,1},{8,4},{69,5},{12,8},{73,9},{16,12},{77,13},{20,16},{8... | collective-permute-start | bytes 1572872 | tf_op jit(solution)/shard_map/ppermute | solution.py:40
  59.0 1.9 %collective-permute-start.7 = (bf16[2,4,2,32,512]{4,3,2,1,0:T(8,128)(2,1)S(1)}, bf16[2,4,2,32,512]{4,3,2,1,0:T(8,128)(2,1)S(1)}, u32[]{:S(2)}, u32[]{:S(2)}) collective-permute-start(bf16[2,4,2,32,512]{4,3,2,1,0:T(8,128)(2,1)S(1)} %bitcast.53), channel_id=1, source_target_pairs={{60,0},{193,1},{0,4},{197,5},{4,8},{201,9},{8,12},{205,13},{12,16}... | collective-permute-start | bytes 1572872 | tf_op jit(solution)/shard_map/ppermute | solution.py:40
  61.0 3.6 %collective-permute-start.5 = (bf16[1,4,2,32,512]{4,3,2,1,0:T(8,128)(2,1)S(1)}, bf16[1,4,2,32,512]{4,3,2,1,0:T(8,128)(2,1)S(1)}, u32[]{:S(2)}, u32[]{:S(2)}) collective-permute-start(bf16[1,4,2,32,512]{4,3,2,1,0:T(8,128)(2,1)S(1)} %get-tuple-element.38), channel_id=1, source_target_pairs={{8,0},{129,1},{12,4},{133,5},{16,8},{137,9},{20,12},{141,13},{24,1... | collective-permute-start | bytes 786440 | tf_op jit(solution)/shard_map/ppermute | solution.py:40
  64.7 3.2 %collective-permute-start.6 = (bf16[1,4,2,32,512]{4,3,2,1,0:T(8,128)(2,1)S(1)}, bf16[1,4,2,32,512]{4,3,2,1,0:T(8,128)(2,1)S(1)}, u32[]{:S(2)}, u32[]{:S(2)}) collective-permute-start(bf16[1,4,2,32,512]{4,3,2,1,0:T(8,128)(2,1)S(1)} %get-tuple-element.37), channel_id=1, source_target_pairs={{56,0},{129,1},{60,4},{133,5},{0,8},{137,9},{4,12},{141,13},{8,16}... | collective-permute-start | bytes 786440 | tf_op jit(solution)/shard_map/ppermute | solution.py:40
  71.2 5.8 %collective-permute-start.2 = (bf16[2,256,2048]{2,1,0:T(8,128)(2,1)}, bf16[2,256,2048]{2,1,0:T(8,128)(2,1)}, u32[]{:S(2)}, u32[]{:S(2)}) collective-permute-start(bf16[2,256,2048]{2,1,0:T(8,128)(2,1)} %pad_maximum_fusion.1), channel_id=1, source_target_pairs={{0,1},{1,0},{2,3},{3,2},{4,5},{5,4},{6,7},{7,6},{8,9},{9,8},{10,11... | collective-permute-start | bytes 6291464 | tf_op jit(solution)/shard_map/ppermute | solution.py:26
  78.5 3.4 %collective-permute-start.9 = (bf16[4,2,4,2,32,256]{5,4,3,2,1,0:T(8,128)(2,1)}, bf16[4,2,4,2,32,256]{5,4,3,2,1,0:T(8,128)(2,1)}, u32[]{:S(2)}, u32[]{:S(2)}) collective-permute-start(bf16[4,2,4,2,32,256]{5,4,3,2,1,0:T(8,128)(2,1)} %get-tuple-element.12.refs_0_), channel_id=1, source_target_pairs={{192,0},{61,1},{196,4},{1,5},{200,8},{5,9},{204,12},{9,13},{208,16... | collective-permute-start | bytes 3145736 | tf_op jit(solution)/shard_map/ppermute | solution.py:40
  81.9 4.6 %collective-permute-start.12 = (bf16[4,2,4,2,32,256]{5,4,3,2,1,0:T(8,128)(2,1)S(1)}, bf16[4,2,4,2,32,256]{5,4,3,2,1,0:T(8,128)(2,1)}, u32[]{:S(2)}, u32[]{:S(2)}) collective-permute-start(bf16[4,2,4,2,32,256]{5,4,3,2,1,0:T(8,128)(2,1)S(1)} %get-tuple-element.14.refs_0_), channel_id=1, source_target_pairs={{64,0},{5,1},{68,4},{9,5},{72,8},{13,9},{76,12},{17,13},{80,16},{2... | collective-permute-start | bytes 3145736 | tf_op jit(solution)/shard_map/ppermute | solution.py:40
  86.5 3.4 %collective-permute-start.8 = (bf16[4,2,4,2,32,256]{5,4,3,2,1,0:T(8,128)(2,1)}, bf16[4,2,4,2,32,256]{5,4,3,2,1,0:T(8,128)(2,1)S(1)}, u32[]{:S(2)}, u32[]{:S(2)}) collective-permute-start(bf16[4,2,4,2,32,256]{5,4,3,2,1,0:T(8,128)(2,1)} %get-tuple-element.12.refs_0_), channel_id=1, source_target_pairs={{64,0},{5,1},{68,4},{9,5},{72,8},{13,9},{76,12},{17,13},{80,16},{2... | collective-permute-start | bytes 3145736 | tf_op jit(solution)/shard_map/ppermute | solution.py:40
  89.9 1.9 %collective-permute-start.14 = (bf16[4,2,4,2,32,256]{5,4,3,2,1,0:T(8,128)(2,1)S(1)}, bf16[4,2,4,2,32,256]{5,4,3,2,1,0:T(8,128)(2,1)S(1)}, u32[]{:S(2)}, u32[]{:S(2)}) collective-permute-start(bf16[4,2,4,2,32,256]{5,4,3,2,1,0:T(8,128)(2,1)S(1)} %get-tuple-element.14.refs_0_), channel_id=1, source_target_pairs={{192,0},{61,1},{196,4},{1,5},{200,8},{5,9},{204,12},{9,13},{208,16... | collective-permute-start | bytes 3145736 | tf_op jit(solution)/shard_map/ppermute | solution.py:40
  91.8 5.5 %collective-permute-done.9.refs_3_ = bf16[4,2,4,2,32,256]{5,4,3,2,1,0:T(8,128)(2,1)} collective-permute-done((bf16[4,2,4,2,32,256]{5,4,3,2,1,0:T(8,128)(2,1)}, bf16[4,2,4,2,32,256]{5,4,3,2,1,0:T(8,128)(2,1)}, u32[]{:S(2)}, u32[]{:S(2)}) %collective-permute-start.9) | collective-permute-done | bytes 1048608 | tf_op jit(solution)/shard_map/ppermute | solution.py:40
  99.2 4.6 %collective-permute-start.13 = (bf16[4,2,4,2,32,256]{5,4,3,2,1,0:T(8,128)(2,1)}, bf16[4,2,4,2,32,256]{5,4,3,2,1,0:T(8,128)(2,1)S(1)}, u32[]{:S(2)}, u32[]{:S(2)}) collective-permute-start(bf16[4,2,4,2,32,256]{5,4,3,2,1,0:T(8,128)(2,1)} %collective-permute-done.12.refs_1_), channel_id=1, source_target_pairs={{64,0},{5,1},{68,4},{9,5},{72,8},{13,9},{76,12},{17,13},{80,16},{2... | collective-permute-start | bytes 3145736 | tf_op jit(solution)/shard_map/ppermute | solution.py:40
  108.4 12.3 %collective-permute-done.13.refs_2_ = bf16[4,2,4,2,32,256]{5,4,3,2,1,0:T(8,128)(2,1)S(1)} collective-permute-done((bf16[4,2,4,2,32,256]{5,4,3,2,1,0:T(8,128)(2,1)}, bf16[4,2,4,2,32,256]{5,4,3,2,1,0:T(8,128)(2,1)S(1)}, u32[]{:S(2)}, u32[]{:S(2)}) %collective-permute-start.13) | collective-permute-done | bytes 1048608 | tf_op jit(solution)/shard_map/ppermute | solution.py:40
  120.8 5.1 %shard_map.68 = bf16[3,512,256]{2,1,0:T(8,128)(2,1)} custom-call(s32[3]{0:T(128)S(1)} %pad_add_fusion.place, bf16[512,2048]{1,0:T(8,128)(2,1)S(1)} %bitcast.44, bf16[512,2048]{1,0:T(8,128)(2,1)S(1)} %bitcast.47, bf16[4,2,4,2,32,256]{5,4,3,2,1,0:T(8,128)(2,1)S(1)} %get-tuple-element.14.refs_0_, ...), custom_call_target="tpu_custom_call" | custom-call | flops 1610612736 | bytes 6291456 | tf_op jit(solution)/shard_map/pallas_call | solution.py:205
  125.9 4.3 %collective-permute-start.15 = (bf16[3,512,256]{2,1,0:T(8,128)(2,1)}, bf16[3,512,256]{2,1,0:T(8,128)(2,1)}, u32[]{:S(2)}, u32[]{:S(2)}) collective-permute-start(bf16[3,512,256]{2,1,0:T(8,128)(2,1)} %shard_map.68), channel_id=1, source_target_pairs={{0,1},{1,0},{2,3},{3,2},{4,5},{5,4},{6,7},{7,6},{8,9},{9,8},{10,11... | collective-permute-start | bytes 2359304 | tf_op jit(solution)/shard_map/ppermute | solution.py:26
  130.2 8.1 %shard_map.67 = (bf16[3,512,256]{2,1,0:T(8,128)(2,1)}, bf16[512,1024]{1,0:T(8,128)(2,1)}, bf16[512,2048]{1,0:T(8,128)(2,1)}) custom-call(s32[3]{0:T(128)S(1)} %pad_add_fusion.place, bf16[512,2048]{1,0:T(8,128)(2,1)S(1)} %bitcast.45, bf16[512,2048]{1,0:T(8,128)(2,1)S(1)} %bitcast.48, bf16[4,2,4,2,32,256]{5,4,3,2,1,0:T(8,128)(2,1)} %get-tuple-element.12.refs_0_, ...), custom_call_target="tpu_custom_call" | custom-call | flops 3221225472 | bytes 6291456 | tf_op jit(solution)/shard_map/pallas_call | solution.py:205
  138.3 1.9 %collective-permute-start.11 = (bf16[3,512,256]{2,1,0:T(8,128)(2,1)}, bf16[3,512,256]{2,1,0:T(8,128)(2,1)}, u32[]{:S(2)}, u32[]{:S(2)}) collective-permute-start(bf16[3,512,256]{2,1,0:T(8,128)(2,1)} %get-tuple-element.13), channel_id=1, source_target_pairs={{0,1},{1,0},{2,3},{3,2},{4,5},{5,4},{6,7},{7,6},{8,9},{9,8},{10,11... | collective-permute-start | bytes 2359304 | tf_op jit(solution)/shard_map/ppermute | solution.py:26
  145.0 4.8 %shard_map.69 = (bf16[512,1024]{1,0:T(8,128)(2,1)}, bf16[512,2048]{1,0:T(8,128)(2,1)}) custom-call(s32[3]{0:T(128)S(1)} %pad_add_fusion.place, bf16[512,2048]{1,0:T(8,128)(2,1)S(1)} %bitcast.46, bf16[512,2048]{1,0:T(8,128)(2,1)S(1)} %bitcast.49, ...), custom_call_target="tpu_custom_call", output_to_operand_aliasing={{0}: (7, {}), {1}: (8, {})} | custom-call | flops 1610612736 | bytes 6291456 | tf_op jit(solution)/shard_map/pallas_call | solution.py:205
  149.9 2.6 %merge.1 = (bf16[512,1024]{1,0:T(8,128)(2,1)}, bf16[512,2048]{1,0:T(8,128)(2,1)}) custom-call(s32[3]{0:T(128)} %copy-done.6, bf16[3,512,256]{2,1,0:T(8,128)(2,1)} %collective-permute-done.11.first, bf16[3,512,256]{2,1,0:T(8,128)(2,1)} %collective-permute-done.15.second, ...), custom_call_target="tpu_custom_call", output_to_operand_aliasing={{0}: (3, {}), {1}: (4, {})} | custom-call | tf_op jit(solution)/shard_map/merge/pallas_call | solution.py:228
  (66 shorter events, 22.5 us)
Async XLA Ops:
  0.6 11.6 %copy-start.7 = (bf16[64,2048]{1,0:T(8,128)(2,1)S(1)}, bf16[64,2048]{1,0:T(8,128)(2,1)}, u32[]{:S(2)}) copy-start(bf16[64,2048]{1,0:T(8,128)(2,1)} %param.4) | copy-start | bytes 786436
  0.6 11.6 %copy-start.10 = (f32[2048]{0:T(1024)S(1)}, f32[2048]{0:T(1024)}, u32[]{:S(2)}) copy-start(f32[2048]{0:T(1024)} %param.6) | copy-start | bytes 24580
  0.7 8.7 %copy-start.8 = (bf16[128,2048]{1,0:T(8,128)(2,1)S(1)}, bf16[128,2048]{1,0:T(8,128)(2,1)}, u32[]{:S(2)}) copy-start(bf16[128,2048]{1,0:T(8,128)(2,1)} %param.5) | copy-start | bytes 1572868
  3.7 8.5 %collective-permute-start = (bf16[72,2048]{1,0:T(8,128)(2,1)S(1)}, bf16[72,2048]{1,0:T(8,128)(2,1)S(1)}, u32[]{:S(2)}, u32[]{:S(2)}) collective-permute-start(bf16[72,2048]{1,0:T(8,128)(2,1)S(1)} %maximum_maximum_fusion), channel_id=1, source_target_pairs={{0,4},{4,0},{8,12},{12,8},{1,5},{5,1},{9,13},{13,9},{2,6},{6,2},{1... | collective-permute-start | bytes 884744 | tf_op jit(solution)/shard_map/ppermute | solution.py:30
  9.4 10.5 %copy-start.9 = (bf16[32,1024]{1,0:T(8,128)(2,1)S(1)}, bf16[32,1024]{1,0:T(8,128)(2,1)}, u32[]{:S(2)}) copy-start(bf16[32,1024]{1,0:T(8,128)(2,1)} %param.7) | copy-start | bytes 196612
  12.5 55.4 %collective-permute-start.1 = (bf16[256,2048]{1,0:T(8,128)(2,1)S(1)}, bf16[256,2048]{1,0:T(8,128)(2,1)}, u32[]{:S(2)}, u32[]{:S(2)}) collective-permute-start(bf16[256,2048]{1,0:T(8,128)(2,1)S(1)} %pad_maximum_fusion.2), channel_id=1, source_target_pairs={{0,2},{2,0},{1,3},{3,1},{4,6},{6,4},{5,7},{7,5},{8,10},{10,8},{9,1... | collective-permute-start | bytes 3145736 | tf_op jit(solution)/shard_map/ppermute | solution.py:26
  19.9 4.4 %collective-permute-start.3 = (bf16[32,512]{1,0:T(8,128)(2,1)S(1)}, bf16[32,512]{1,0:T(8,128)(2,1)S(1)}, u32[]{:S(2)}, u32[]{:S(2)}) collective-permute-start(bf16[32,512]{1,0:T(8,128)(2,1)S(1)} %get-tuple-element.44), channel_id=1, source_target_pairs={{0,1},{1,0},{2,3},{3,2},{4,5},{5,4},{6,7},{7,6},{8,9},{9,8},{10,11... | collective-permute-start | bytes 98312 | tf_op jit(solution)/shard_map/ppermute | solution.py:26
  54.7 22.4 %collective-permute-start.4 = (bf16[2,4,2,32,512]{4,3,2,1,0:T(8,128)(2,1)S(1)}, bf16[2,4,2,32,512]{4,3,2,1,0:T(8,128)(2,1)S(1)}, u32[]{:S(2)}, u32[]{:S(2)}) collective-permute-start(bf16[2,4,2,32,512]{4,3,2,1,0:T(8,128)(2,1)S(1)} %bitcast.52), channel_id=1, source_target_pairs={{4,0},{65,1},{8,4},{69,5},{12,8},{73,9},{16,12},{77,13},{20,16},{8... | collective-permute-start | bytes 1572872 | tf_op jit(solution)/shard_map/ppermute | solution.py:40
  59.0 18.1 %collective-permute-start.7 = (bf16[2,4,2,32,512]{4,3,2,1,0:T(8,128)(2,1)S(1)}, bf16[2,4,2,32,512]{4,3,2,1,0:T(8,128)(2,1)S(1)}, u32[]{:S(2)}, u32[]{:S(2)}) collective-permute-start(bf16[2,4,2,32,512]{4,3,2,1,0:T(8,128)(2,1)S(1)} %bitcast.53), channel_id=1, source_target_pairs={{60,0},{193,1},{0,4},{197,5},{4,8},{201,9},{8,12},{205,13},{12,16}... | collective-permute-start | bytes 1572872 | tf_op jit(solution)/shard_map/ppermute | solution.py:40
  61.0 15.9 %collective-permute-start.5 = (bf16[1,4,2,32,512]{4,3,2,1,0:T(8,128)(2,1)S(1)}, bf16[1,4,2,32,512]{4,3,2,1,0:T(8,128)(2,1)S(1)}, u32[]{:S(2)}, u32[]{:S(2)}) collective-permute-start(bf16[1,4,2,32,512]{4,3,2,1,0:T(8,128)(2,1)S(1)} %get-tuple-element.38), channel_id=1, source_target_pairs={{8,0},{129,1},{12,4},{133,5},{16,8},{137,9},{20,12},{141,13},{24,1... | collective-permute-start | bytes 786440 | tf_op jit(solution)/shard_map/ppermute | solution.py:40
  64.7 12.3 %collective-permute-start.6 = (bf16[1,4,2,32,512]{4,3,2,1,0:T(8,128)(2,1)S(1)}, bf16[1,4,2,32,512]{4,3,2,1,0:T(8,128)(2,1)S(1)}, u32[]{:S(2)}, u32[]{:S(2)}) collective-permute-start(bf16[1,4,2,32,512]{4,3,2,1,0:T(8,128)(2,1)S(1)} %get-tuple-element.37), channel_id=1, source_target_pairs={{56,0},{129,1},{60,4},{133,5},{0,8},{137,9},{4,12},{141,13},{8,16}... | collective-permute-start | bytes 786440 | tf_op jit(solution)/shard_map/ppermute | solution.py:40
  71.2 32.7 %collective-permute-start.2 = (bf16[2,256,2048]{2,1,0:T(8,128)(2,1)}, bf16[2,256,2048]{2,1,0:T(8,128)(2,1)}, u32[]{:S(2)}, u32[]{:S(2)}) collective-permute-start(bf16[2,256,2048]{2,1,0:T(8,128)(2,1)} %pad_maximum_fusion.1), channel_id=1, source_target_pairs={{0,1},{1,0},{2,3},{3,2},{4,5},{5,4},{6,7},{7,6},{8,9},{9,8},{10,11... | collective-permute-start | bytes 6291464 | tf_op jit(solution)/shard_map/ppermute | solution.py:26
  78.5 18.8 %collective-permute-start.9 = (bf16[4,2,4,2,32,256]{5,4,3,2,1,0:T(8,128)(2,1)}, bf16[4,2,4,2,32,256]{5,4,3,2,1,0:T(8,128)(2,1)}, u32[]{:S(2)}, u32[]{:S(2)}) collective-permute-start(bf16[4,2,4,2,32,256]{5,4,3,2,1,0:T(8,128)(2,1)} %get-tuple-element.12.refs_0_), channel_id=1, source_target_pairs={{192,0},{61,1},{196,4},{1,5},{200,8},{5,9},{204,12},{9,13},{208,16... | collective-permute-start | bytes 3145736 | tf_op jit(solution)/shard_map/ppermute | solution.py:40
  81.9 17.4 %collective-permute-start.12 = (bf16[4,2,4,2,32,256]{5,4,3,2,1,0:T(8,128)(2,1)S(1)}, bf16[4,2,4,2,32,256]{5,4,3,2,1,0:T(8,128)(2,1)}, u32[]{:S(2)}, u32[]{:S(2)}) collective-permute-start(bf16[4,2,4,2,32,256]{5,4,3,2,1,0:T(8,128)(2,1)S(1)} %get-tuple-element.14.refs_0_), channel_id=1, source_target_pairs={{64,0},{5,1},{68,4},{9,5},{72,8},{13,9},{76,12},{17,13},{80,16},{2... | collective-permute-start | bytes 3145736 | tf_op jit(solution)/shard_map/ppermute | solution.py:40
  86.5 54.4 %copy-start.6 = (s32[3]{0:T(128)}, s32[3]{0:T(128)S(1)}, u32[]{:S(2)}) copy-start(s32[3]{0:T(128)S(1)} %pad_add_fusion.place) | copy-start | bytes 40
  86.5 43.7 %collective-permute-start.8 = (bf16[4,2,4,2,32,256]{5,4,3,2,1,0:T(8,128)(2,1)}, bf16[4,2,4,2,32,256]{5,4,3,2,1,0:T(8,128)(2,1)S(1)}, u32[]{:S(2)}, u32[]{:S(2)}) collective-permute-start(bf16[4,2,4,2,32,256]{5,4,3,2,1,0:T(8,128)(2,1)} %get-tuple-element.12.refs_0_), channel_id=1, source_target_pairs={{64,0},{5,1},{68,4},{9,5},{72,8},{13,9},{76,12},{17,13},{80,16},{2... | collective-permute-start | bytes 3145736 | tf_op jit(solution)/shard_map/ppermute | solution.py:40
  89.9 18.5 %collective-permute-start.14 = (bf16[4,2,4,2,32,256]{5,4,3,2,1,0:T(8,128)(2,1)S(1)}, bf16[4,2,4,2,32,256]{5,4,3,2,1,0:T(8,128)(2,1)S(1)}, u32[]{:S(2)}, u32[]{:S(2)}) collective-permute-start(bf16[4,2,4,2,32,256]{5,4,3,2,1,0:T(8,128)(2,1)S(1)} %get-tuple-element.14.refs_0_), channel_id=1, source_target_pairs={{192,0},{61,1},{196,4},{1,5},{200,8},{5,9},{204,12},{9,13},{208,16... | collective-permute-start | bytes 3145736 | tf_op jit(solution)/shard_map/ppermute | solution.py:40
  97.3 32.9 %collective-permute-start.10 = (bf16[4,2,4,2,32,256]{5,4,3,2,1,0:T(8,128)(2,1)}, bf16[4,2,4,2,32,256]{5,4,3,2,1,0:T(8,128)(2,1)S(1)}, u32[]{:S(2)}, u32[]{:S(2)}) collective-permute-start(bf16[4,2,4,2,32,256]{5,4,3,2,1,0:T(8,128)(2,1)} %collective-permute-done.9.refs_3_), channel_id=1, source_target_pairs={{192,0},{61,1},{196,4},{1,5},{200,8},{5,9},{204,12},{9,13},{208,16... | collective-permute-start | bytes 3145736 | tf_op jit(solution)/shard_map/ppermute | solution.py:40
  99.2 21.5 %collective-permute-start.13 = (bf16[4,2,4,2,32,256]{5,4,3,2,1,0:T(8,128)(2,1)}, bf16[4,2,4,2,32,256]{5,4,3,2,1,0:T(8,128)(2,1)S(1)}, u32[]{:S(2)}, u32[]{:S(2)}) collective-permute-start(bf16[4,2,4,2,32,256]{5,4,3,2,1,0:T(8,128)(2,1)} %collective-permute-done.12.refs_1_), channel_id=1, source_target_pairs={{64,0},{5,1},{68,4},{9,5},{72,8},{13,9},{76,12},{17,13},{80,16},{2... | collective-permute-start | bytes 3145736 | tf_op jit(solution)/shard_map/ppermute | solution.py:40
  106.6 23.6 %copy-start = (bf16[4,128,2048]{2,1,0:T(8,128)(2,1)}, bf16[4,128,2048]{2,1,0:T(8,128)(2,1)S(1)}, u32[]{:S(2)}) copy-start(bf16[4,128,2048]{2,1,0:T(8,128)(2,1)S(1)} %get-tuple-element.21) | copy-start | bytes 6291460
  108.4 17.5 %copy-start.2 = (bf16[4,2,4,2,32,256]{5,4,3,2,1,0:T(8,128)(2,1)}, bf16[4,2,4,2,32,256]{5,4,3,2,1,0:T(8,128)(2,1)S(1)}, u32[]{:S(2)}) copy-start(bf16[4,2,4,2,32,256]{5,4,3,2,1,0:T(8,128)(2,1)S(1)} %collective-permute-done.14.refs_3_) | copy-start | bytes 3145732
  120.8 5.1 %copy-start.4 = (bf16[4,2,4,2,32,256]{5,4,3,2,1,0:T(8,128)(2,1)}, bf16[4,2,4,2,32,256]{5,4,3,2,1,0:T(8,128)(2,1)S(1)}, u32[]{:S(2)}) copy-start(bf16[4,2,4,2,32,256]{5,4,3,2,1,0:T(8,128)(2,1)S(1)} %collective-permute-done.13.refs_2_) | copy-start | bytes 3145732
  125.9 23.9 %collective-permute-start.15 = (bf16[3,512,256]{2,1,0:T(8,128)(2,1)}, bf16[3,512,256]{2,1,0:T(8,128)(2,1)}, u32[]{:S(2)}, u32[]{:S(2)}) collective-permute-start(bf16[3,512,256]{2,1,0:T(8,128)(2,1)} %shard_map.68), channel_id=1, source_target_pairs={{0,1},{1,0},{2,3},{3,2},{4,5},{5,4},{6,7},{7,6},{8,9},{9,8},{10,11... | collective-permute-start | bytes 2359304 | tf_op jit(solution)/shard_map/ppermute | solution.py:26
  138.3 11.5 %collective-permute-start.11 = (bf16[3,512,256]{2,1,0:T(8,128)(2,1)}, bf16[3,512,256]{2,1,0:T(8,128)(2,1)}, u32[]{:S(2)}, u32[]{:S(2)}) collective-permute-start(bf16[3,512,256]{2,1,0:T(8,128)(2,1)} %get-tuple-element.13), channel_id=1, source_target_pairs={{0,1},{1,0},{2,3},{3,2},{4,5},{5,4},{6,7},{7,6},{8,9},{9,8},{10,11... | collective-permute-start | bytes 2359304 | tf_op jit(solution)/shard_map/ppermute | solution.py:26
  (3 other events, 4.0 us)

commit v2 on v1

--- a/solution.py
+++ b/solution.py
@@ -151,10 +151,13 @@
 
 
 def part_kernel(number, given, own, n_in, place, vlm, action, *refs):
-    slabs, refs = refs[:4], list(refs[n_in:])
+    slabs, before, refs = refs[:4], refs[4:n_in], list(refs[n_in:])
     given_out = refs.pop(0) if given else None
     vlm_out, action_out = (refs.pop(0), refs.pop(0)) if own else (None, None)
     weights, stage, sems, out_sems = refs
+    more = column_copies(number - 1, 1 - place[2], before[0], vlm_out, action_out, out_sems.at[1]) if before else []
+    for copy in more:
+        copy.start()
     jobs = [1] * given + [0] * own
     copies = [weight_copies(place, core, slabs, weights.at[n], sems.at[n]) for n, core in enumerate(jobs)]
     for job in copies:
@@ -164,7 +167,7 @@
         for copy in copies[n]:
             copy.wait()
         target = given_out if core else stage
-        outs = [] if core else column_copies(number, place[2], stage, vlm_out, action_out, out_sems)
+        outs = [] if core else column_copies(number, place[2], stage, vlm_out, action_out, out_sems.at[0])
 
         def store(block, i, values, target=target, outs=outs):
             target[block, i : i + ROWS, :] = values
@@ -174,13 +177,13 @@
         products(place, vlm, action, weights.at[n], store)
         for copy in outs:
             copy.wait()
-
-
-def merge_kernel(place, first, second, vlm_in, action_in, vlm_out, action_out, sems):
+    for copy in more:
+        copy.wait()
+
+
+def merge_kernel(place, parts, vlm_in, action_in, vlm_out, action_out, sems):
     del vlm_in, action_in
-    copies = []
-    for number, parts in enumerate((first, second)):
-        copies += column_copies(number, 1 - place[2], parts, vlm_out, action_out, sems.at[number])
+    copies = column_copies(1, 1 - place[2], parts, vlm_out, action_out, sems)
     for copy in copies:
         copy.start()
     for copy in copies:
@@ -205,15 +208,15 @@
         return pl.pallas_call(
             kernel,
             out_shape=(taken,) * given + wide * own,
-            in_specs=[SMEM, VMEM, VMEM] + [HBM] * n_in,
+            in_specs=[SMEM, VMEM, VMEM] + [HBM] * 4 + [VMEM, HBM, HBM][: len(before)],
             out_specs=(VMEM,) * given + (HBM, HBM) * own,
             scratch_shapes=[
                 pltpu.VMEM((jobs, 2, NX, NU, 2, rows, 2 * part), jnp.bfloat16),
                 pltpu.VMEM(taken.shape, taken.dtype),
                 pltpu.SemaphoreType.DMA((jobs, 32)),
-                pltpu.SemaphoreType.DMA((3,)),
+                pltpu.SemaphoreType.DMA((2, 3)),
             ],
-            input_output_aliases={7 + i: given + i for i in range(len(before))},
+            input_output_aliases={7 + i: i - 1 for i in range(1, len(before))},
             compiler_params=pltpu.CompilerParams(vmem_limit_bytes=14 * 1024 * 1024),
             cost_estimate=pl.CostEstimate(
                 flops=6 * count * depth * part * jobs, bytes_accessed=6 * 1024 * 1024, transcendentals=0
@@ -224,16 +227,16 @@
     taken_low = swap(given_low, "c")
     (given_high,) = call(1, 1, 0)
     taken_high = swap(given_high, "c")
-    wide_own = call(1, 0, 1, tuple(wide_low))
+    wide_own = call(1, 0, 1, (taken_low, *wide_low))
     return pl.pallas_call(
         merge_kernel,
         out_shape=wide,
-        in_specs=[SMEM, VMEM, VMEM, HBM, HBM],
+        in_specs=[SMEM, VMEM, HBM, HBM],
         out_specs=(HBM, HBM),
-        scratch_shapes=[pltpu.SemaphoreType.DMA((2, 3))],
-        input_output_aliases={3: 0, 4: 1},
+        scratch_shapes=[pltpu.SemaphoreType.DMA((3,))],
+        input_output_aliases={2: 0, 3: 1},
         name="merge",
-    )(place, taken_low, taken_high, *wide_own)
+    )(place, taken_high, *wide_own)
 
 
 def local(vlm_tokens, action_tokens, norm_gain, proj_old):

time: 155 us -> 153 us (0.987)
  no operation moved by 1% of the time
where the time goes in v2:
time: 153 us; the launch traced here: 151 us
  starting transfers between devices  59.1 us (39%)
  blocking collectives  30.4 us (20%)
  waiting for transfers between devices  21.1 us (14%)
  Pallas kernels  20.8 us (14%)
  other arithmetic  12.2 us (8%)
  local copies, waits for them, and re-layouts  5.82 us (4%)
    ppermute x10, starting transfers between devices, along(): return lax.ppermute(array, PLANE, pairs)  32.8 us
    all_gather x1, blocking collectives, near_weight(): mates = lax.all_gather(jnp.stack([mine, taken]), 'u')  24.5 us
    ppermute x5, starting transfers between devices, swap(): return lax.ppermute(array, axis, [(0, 1), (1, 0)])  22 us
    pallas_call x3, Pallas kernels, call(): pl.pallas_call(kernel, out_shape=(taken,) * given + wide * own, in_specs=...  18.8 us
    ppermute x10, waiting for transfers between devices, along(): return lax.ppermute(array, PLANE, pairs)  18.4 us
    all_gather x1, blocking collectives, near_weight(): planes = lax.all_gather(mates, 'y')  5.87 us
    ppermute x1, starting transfers between devices, swap_parity(): return lax.ppermute(array, 'w', [(i, i ^ 1) for i in range(NW)])  4.36 us
    unnamed x23, local copies, waits for them, and re-layouts  4.1 us
  transfers between devices with their start and end apart: 16, of which 5 were waited for; matrix products, arithmetic and copies ran while one was open for 7% of the time, Pallas kernels for 12%

profile of v2, /device:TPU:1, one launch (start us, length us, event | category | flops | bytes accessed | tf_op | source)
XLA Modules:
  0.0 150.7 jit_solution(16928425617897136145)
XLA Ops:
  3.7 4.4 %collective-permute-start = (bf16[72,2048]{1,0:T(8,128)(2,1)S(1)}, bf16[72,2048]{1,0:T(8,128)(2,1)S(1)}, u32[]{:S(2)}, u32[]{:S(2)}) collective-permute-start(bf16[72,2048]{1,0:T(8,128)(2,1)S(1)} %maximum_maximum_fusion), channel_id=1, source_target_pairs={{0,4},{4,0},{8,12},{12,8},{1,5},{5,1},{9,13},{13,9},{2,6},{6,2},{1... | collective-permute-start | bytes 884744 | tf_op jit(solution)/shard_map/ppermute | solution.py:30
  12.5 7.3 %collective-permute-start.1 = (bf16[256,2048]{1,0:T(8,128)(2,1)S(1)}, bf16[256,2048]{1,0:T(8,128)(2,1)}, u32[]{:S(2)}, u32[]{:S(2)}) collective-permute-start(bf16[256,2048]{1,0:T(8,128)(2,1)S(1)} %pad_maximum_fusion.2), channel_id=1, source_target_pairs={{0,2},{2,0},{1,3},{3,1},{4,6},{6,4},{5,7},{7,5},{8,10},{10,8},{9,1... | collective-permute-start | bytes 3145736 | tf_op jit(solution)/shard_map/ppermute | solution.py:26
  19.9 3.5 %collective-permute-start.3 = (bf16[32,512]{1,0:T(8,128)(2,1)S(1)}, bf16[32,512]{1,0:T(8,128)(2,1)S(1)}, u32[]{:S(2)}, u32[]{:S(2)}) collective-permute-start(bf16[32,512]{1,0:T(8,128)(2,1)S(1)} %get-tuple-element.44), channel_id=1, source_target_pairs={{0,1},{1,0},{2,3},{3,2},{4,5},{5,4},{6,7},{7,6},{8,9},{9,8},{10,11... | collective-permute-start | bytes 98312 | tf_op jit(solution)/shard_map/ppermute | solution.py:26
  24.3 24.5 %all-gather = bf16[8,32,512]{2,1,0:T(8,128)(2,1)S(1)} all-gather(bf16[2,32,512]{2,1,0:T(8,128)(2,1)S(1)} %pad_maximum_fusion.5), channel_id=2, replica_groups=mesh['y'=2,'x'=4,'u'=4,'w'=4,'h'=2,'c'=2] {'u'}, dimensions={0}, use_global_device_ids=true | all-gather | bytes 327680 | tf_op jit(solution)/shard_map/all_gather | solution.py:55
  48.8 5.9 %all-gather.1 = bf16[8,2,32,512]{3,2,1,0:T(8,128)(2,1)S(1)} all-gather(bf16[4,2,32,512]{3,2,1,0:T(8,128)(2,1)S(1)} %bitcast.55), channel_id=3, replica_groups=mesh['y'=2,'x'=4,'u'=4,'w'=4,'h'=2,'c'=2] {'y'}, dimensions={0}, use_global_device_ids=true | all-gather | bytes 786432 | tf_op jit(solution)/shard_map/all_gather | solution.py:56
  54.7 4.4 %collective-permute-start.4 = (bf16[2,4,2,32,512]{4,3,2,1,0:T(8,128)(2,1)S(1)}, bf16[2,4,2,32,512]{4,3,2,1,0:T(8,128)(2,1)S(1)}, u32[]{:S(2)}, u32[]{:S(2)}) collective-permute-start(bf16[2,4,2,32,512]{4,3,2,1,0:T(8,128)(2,1)S(1)} %bitcast.52), channel_id=1, source_target_pairs={{4,0},{65,1},{8,4},{69,5},{12,8},{73,9},{16,12},{77,13},{20,16},{8... | collective-permute-start | bytes 1572872 | tf_op jit(solution)/shard_map/ppermute | solution.py:40
  59.0 1.9 %collective-permute-start.7 = (bf16[2,4,2,32,512]{4,3,2,1,0:T(8,128)(2,1)S(1)}, bf16[2,4,2,32,512]{4,3,2,1,0:T(8,128)(2,1)S(1)}, u32[]{:S(2)}, u32[]{:S(2)}) collective-permute-start(bf16[2,4,2,32,512]{4,3,2,1,0:T(8,128)(2,1)S(1)} %bitcast.53), channel_id=1, source_target_pairs={{60,0},{193,1},{0,4},{197,5},{4,8},{201,9},{8,12},{205,13},{12,16}... | collective-permute-start | bytes 1572872 | tf_op jit(solution)/shard_map/ppermute | solution.py:40
  61.0 3.6 %collective-permute-start.5 = (bf16[1,4,2,32,512]{4,3,2,1,0:T(8,128)(2,1)S(1)}, bf16[1,4,2,32,512]{4,3,2,1,0:T(8,128)(2,1)S(1)}, u32[]{:S(2)}, u32[]{:S(2)}) collective-permute-start(bf16[1,4,2,32,512]{4,3,2,1,0:T(8,128)(2,1)S(1)} %get-tuple-element.38), channel_id=1, source_target_pairs={{8,0},{129,1},{12,4},{133,5},{16,8},{137,9},{20,12},{141,13},{24,1... | collective-permute-start | bytes 786440 | tf_op jit(solution)/shard_map/ppermute | solution.py:40
  64.7 3.2 %collective-permute-start.6 = (bf16[1,4,2,32,512]{4,3,2,1,0:T(8,128)(2,1)S(1)}, bf16[1,4,2,32,512]{4,3,2,1,0:T(8,128)(2,1)S(1)}, u32[]{:S(2)}, u32[]{:S(2)}) collective-permute-start(bf16[1,4,2,32,512]{4,3,2,1,0:T(8,128)(2,1)S(1)} %get-tuple-element.37), channel_id=1, source_target_pairs={{56,0},{129,1},{60,4},{133,5},{0,8},{137,9},{4,12},{141,13},{8,16}... | collective-permute-start | bytes 786440 | tf_op jit(solution)/shard_map/ppermute | solution.py:40
  71.2 5.8 %collective-permute-start.2 = (bf16[2,256,2048]{2,1,0:T(8,128)(2,1)}, bf16[2,256,2048]{2,1,0:T(8,128)(2,1)}, u32[]{:S(2)}, u32[]{:S(2)}) collective-permute-start(bf16[2,256,2048]{2,1,0:T(8,128)(2,1)} %pad_maximum_fusion.1), channel_id=1, source_target_pairs={{0,1},{1,0},{2,3},{3,2},{4,5},{5,4},{6,7},{7,6},{8,9},{9,8},{10,11... | collective-permute-start | bytes 6291464 | tf_op jit(solution)/shard_map/ppermute | solution.py:26
  78.5 3.4 %collective-permute-start.13 = (bf16[4,2,4,2,32,256]{5,4,3,2,1,0:T(8,128)(2,1)}, bf16[4,2,4,2,32,256]{5,4,3,2,1,0:T(8,128)(2,1)}, u32[]{:S(2)}, u32[]{:S(2)}) collective-permute-start(bf16[4,2,4,2,32,256]{5,4,3,2,1,0:T(8,128)(2,1)} %get-tuple-element.13.refs_0_), channel_id=1, source_target_pairs={{192,0},{61,1},{196,4},{1,5},{200,8},{5,9},{204,12},{9,13},{208,16... | collective-permute-start | bytes 3145736 | tf_op jit(solution)/shard_map/ppermute | solution.py:40
  81.9 4.6 %collective-permute-start.8 = (bf16[4,2,4,2,32,256]{5,4,3,2,1,0:T(8,128)(2,1)S(1)}, bf16[4,2,4,2,32,256]{5,4,3,2,1,0:T(8,128)(2,1)}, u32[]{:S(2)}, u32[]{:S(2)}) collective-permute-start(bf16[4,2,4,2,32,256]{5,4,3,2,1,0:T(8,128)(2,1)S(1)} %get-tuple-element.12.refs_0_), channel_id=1, source_target_pairs={{64,0},{5,1},{68,4},{9,5},{72,8},{13,9},{76,12},{17,13},{80,16},{2... | collective-permute-start | bytes 3145736 | tf_op jit(solution)/shard_map/ppermute | solution.py:40
  86.5 3.4 %collective-permute-start.12 = (bf16[4,2,4,2,32,256]{5,4,3,2,1,0:T(8,128)(2,1)}, bf16[4,2,4,2,32,256]{5,4,3,2,1,0:T(8,128)(2,1)S(1)}, u32[]{:S(2)}, u32[]{:S(2)}) collective-permute-start(bf16[4,2,4,2,32,256]{5,4,3,2,1,0:T(8,128)(2,1)} %get-tuple-element.13.refs_0_), channel_id=1, source_target_pairs={{64,0},{5,1},{68,4},{9,5},{72,8},{13,9},{76,12},{17,13},{80,16},{2... | collective-permute-start | bytes 3145736 | tf_op jit(solution)/shard_map/ppermute | solution.py:40
  89.9 1.9 %collective-permute-start.10 = (bf16[4,2,4,2,32,256]{5,4,3,2,1,0:T(8,128)(2,1)S(1)}, bf16[4,2,4,2,32,256]{5,4,3,2,1,0:T(8,128)(2,1)S(1)}, u32[]{:S(2)}, u32[]{:S(2)}) collective-permute-start(bf16[4,2,4,2,32,256]{5,4,3,2,1,0:T(8,128)(2,1)S(1)} %get-tuple-element.12.refs_0_), channel_id=1, source_target_pairs={{192,0},{61,1},{196,4},{1,5},{200,8},{5,9},{204,12},{9,13},{208,16... | collective-permute-start | bytes 3145736 | tf_op jit(solution)/shard_map/ppermute | solution.py:40
  91.8 5.5 %collective-permute-done.13.refs_3_ = bf16[4,2,4,2,32,256]{5,4,3,2,1,0:T(8,128)(2,1)} collective-permute-done((bf16[4,2,4,2,32,256]{5,4,3,2,1,0:T(8,128)(2,1)}, bf16[4,2,4,2,32,256]{5,4,3,2,1,0:T(8,128)(2,1)}, u32[]{:S(2)}, u32[]{:S(2)}) %collective-permute-start.13) | collective-permute-done | bytes 1048608 | tf_op jit(solution)/shard_map/ppermute | solution.py:40
  99.2 4.6 %collective-permute-start.9 = (bf16[4,2,4,2,32,256]{5,4,3,2,1,0:T(8,128)(2,1)}, bf16[4,2,4,2,32,256]{5,4,3,2,1,0:T(8,128)(2,1)S(1)}, u32[]{:S(2)}, u32[]{:S(2)}) collective-permute-start(bf16[4,2,4,2,32,256]{5,4,3,2,1,0:T(8,128)(2,1)} %collective-permute-done.8.refs_1_), channel_id=1, source_target_pairs={{64,0},{5,1},{68,4},{9,5},{72,8},{13,9},{76,12},{17,13},{80,16},{2... | collective-permute-start | bytes 3145736 | tf_op jit(solution)/shard_map/ppermute | solution.py:40
  106.8 2.7 %collective-permute-done.12.refs_1_ = bf16[4,2,4,2,32,256]{5,4,3,2,1,0:T(8,128)(2,1)S(1)} collective-permute-done((bf16[4,2,4,2,32,256]{5,4,3,2,1,0:T(8,128)(2,1)}, bf16[4,2,4,2,32,256]{5,4,3,2,1,0:T(8,128)(2,1)S(1)}, u32[]{:S(2)}, u32[]{:S(2)}) %collective-permute-start.12) | collective-permute-done | bytes 1048608 | tf_op jit(solution)/shard_map/ppermute | solution.py:40
  109.5 10.1 %collective-permute-done.14.refs_2_ = bf16[4,2,4,2,32,256]{5,4,3,2,1,0:T(8,128)(2,1)S(1)} collective-permute-done((bf16[4,2,4,2,32,256]{5,4,3,2,1,0:T(8,128)(2,1)}, bf16[4,2,4,2,32,256]{5,4,3,2,1,0:T(8,128)(2,1)S(1)}, u32[]{:S(2)}, u32[]{:S(2)}) %collective-permute-start.14) | collective-permute-done | bytes 1048608 | tf_op jit(solution)/shard_map/ppermute | solution.py:40
  119.7 8.2 %shard_map.68 = (bf16[3,512,256]{2,1,0:T(8,128)(2,1)}, bf16[512,1024]{1,0:T(8,128)(2,1)}, bf16[512,2048]{1,0:T(8,128)(2,1)}) custom-call(s32[3]{0:T(128)S(1)} %pad_add_fusion.place, bf16[512,2048]{1,0:T(8,128)(2,1)S(1)} %bitcast.44, bf16[512,2048]{1,0:T(8,128)(2,1)S(1)} %bitcast.47, bf16[4,2,4,2,32,256]{5,4,3,2,1,0:T(8,128)(2,1)} %get-tuple-element.13.refs_0_, ...), custom_call_target="tpu_custom_call" | custom-call | flops 3221225472 | bytes 6291456 | tf_op jit(solution)/shard_map/pallas_call | solution.py:208
  127.9 3.4 %collective-permute-start.15 = (bf16[3,512,256]{2,1,0:T(8,128)(2,1)}, bf16[3,512,256]{2,1,0:T(8,128)(2,1)}, u32[]{:S(2)}, u32[]{:S(2)}) collective-permute-start(bf16[3,512,256]{2,1,0:T(8,128)(2,1)} %get-tuple-element.14), channel_id=1, source_target_pairs={{0,1},{1,0},{2,3},{3,2},{4,5},{5,4},{6,7},{7,6},{8,9},{9,8},{10,11... | collective-permute-start | bytes 2359304 | tf_op jit(solution)/shard_map/ppermute | solution.py:26
  131.3 5.1 %shard_map.67 = bf16[3,512,256]{2,1,0:T(8,128)(2,1)} custom-call(s32[3]{0:T(128)S(1)} %pad_add_fusion.place, bf16[512,2048]{1,0:T(8,128)(2,1)S(1)} %bitcast.45, bf16[512,2048]{1,0:T(8,128)(2,1)S(1)} %bitcast.48, bf16[4,2,4,2,32,256]{5,4,3,2,1,0:T(8,128)(2,1)S(1)} %get-tuple-element.12.refs_0_, ...), custom_call_target="tpu_custom_call" | custom-call | flops 1610612736 | bytes 6291456 | tf_op jit(solution)/shard_map/pallas_call | solution.py:208
  136.4 1.9 %collective-permute-start.11 = (bf16[3,512,256]{2,1,0:T(8,128)(2,1)}, bf16[3,512,256]{2,1,0:T(8,128)(2,1)}, u32[]{:S(2)}, u32[]{:S(2)}) collective-permute-start(bf16[3,512,256]{2,1,0:T(8,128)(2,1)} %shard_map.67), channel_id=1, source_target_pairs={{0,1},{1,0},{2,3},{3,2},{4,5},{5,4},{6,7},{7,6},{8,9},{9,8},{10,11... | collective-permute-start | bytes 2359304 | tf_op jit(solution)/shard_map/ppermute | solution.py:26
  143.1 5.5 %shard_map.69 = (bf16[512,1024]{1,0:T(8,128)(2,1)}, bf16[512,2048]{1,0:T(8,128)(2,1)}) custom-call(s32[3]{0:T(128)S(1)} %pad_add_fusion.place, bf16[512,2048]{1,0:T(8,128)(2,1)S(1)} %bitcast.46, bf16[512,2048]{1,0:T(8,128)(2,1)S(1)} %bitcast.49, ...), custom_call_target="tpu_custom_call", output_to_operand_aliasing={{0}: (8, {}), {1}: (9, {})} | custom-call | flops 1610612736 | bytes 6291456 | tf_op jit(solution)/shard_map/pallas_call | solution.py:208
  148.6 2.1 %merge.1 = (bf16[512,1024]{1,0:T(8,128)(2,1)}, bf16[512,2048]{1,0:T(8,128)(2,1)}) custom-call(s32[3]{0:T(128)} %copy-done.6, bf16[3,512,256]{2,1,0:T(8,128)(2,1)} %collective-permute-done.11.parts, bf16[512,1024]{1,0:T(8,128)(2,1)} %get-tuple-element.17.vlm_in, ...), custom_call_target="tpu_custom_call", output_to_operand_aliasing={{0}: (2, {}), {1}: (3, {})} | custom-call | tf_op jit(solution)/shard_map/merge/pallas_call | solution.py:231
  (66 shorter events, 22.7 us)
Async XLA Ops:
  0.6 11.6 %copy-start.7 = (bf16[64,2048]{1,0:T(8,128)(2,1)S(1)}, bf16[64,2048]{1,0:T(8,128)(2,1)}, u32[]{:S(2)}) copy-start(bf16[64,2048]{1,0:T(8,128)(2,1)} %param.4) | copy-start | bytes 786436
  0.6 11.6 %copy-start.10 = (f32[2048]{0:T(1024)S(1)}, f32[2048]{0:T(1024)}, u32[]{:S(2)}) copy-start(f32[2048]{0:T(1024)} %param.6) | copy-start | bytes 24580
  0.7 8.7 %copy-start.8 = (bf16[128,2048]{1,0:T(8,128)(2,1)S(1)}, bf16[128,2048]{1,0:T(8,128)(2,1)}, u32[]{:S(2)}) copy-start(bf16[128,2048]{1,0:T(8,128)(2,1)} %param.5) | copy-start | bytes 1572868
  3.7 8.5 %collective-permute-start = (bf16[72,2048]{1,0:T(8,128)(2,1)S(1)}, bf16[72,2048]{1,0:T(8,128)(2,1)S(1)}, u32[]{:S(2)}, u32[]{:S(2)}) collective-permute-start(bf16[72,2048]{1,0:T(8,128)(2,1)S(1)} %maximum_maximum_fusion), channel_id=1, source_target_pairs={{0,4},{4,0},{8,12},{12,8},{1,5},{5,1},{9,13},{13,9},{2,6},{6,2},{1... | collective-permute-start | bytes 884744 | tf_op jit(solution)/shard_map/ppermute | solution.py:30
  9.4 10.5 %copy-start.9 = (bf16[32,1024]{1,0:T(8,128)(2,1)S(1)}, bf16[32,1024]{1,0:T(8,128)(2,1)}, u32[]{:S(2)}) copy-start(bf16[32,1024]{1,0:T(8,128)(2,1)} %param.7) | copy-start | bytes 196612
  12.5 55.4 %collective-permute-start.1 = (bf16[256,2048]{1,0:T(8,128)(2,1)S(1)}, bf16[256,2048]{1,0:T(8,128)(2,1)}, u32[]{:S(2)}, u32[]{:S(2)}) collective-permute-start(bf16[256,2048]{1,0:T(8,128)(2,1)S(1)} %pad_maximum_fusion.2), channel_id=1, source_target_pairs={{0,2},{2,0},{1,3},{3,1},{4,6},{6,4},{5,7},{7,5},{8,10},{10,8},{9,1... | collective-permute-start | bytes 3145736 | tf_op jit(solution)/shard_map/ppermute | solution.py:26
  19.9 4.4 %collective-permute-start.3 = (bf16[32,512]{1,0:T(8,128)(2,1)S(1)}, bf16[32,512]{1,0:T(8,128)(2,1)S(1)}, u32[]{:S(2)}, u32[]{:S(2)}) collective-permute-start(bf16[32,512]{1,0:T(8,128)(2,1)S(1)} %get-tuple-element.44), channel_id=1, source_target_pairs={{0,1},{1,0},{2,3},{3,2},{4,5},{5,4},{6,7},{7,6},{8,9},{9,8},{10,11... | collective-permute-start | bytes 98312 | tf_op jit(solution)/shard_map/ppermute | solution.py:26
  54.7 22.4 %collective-permute-start.4 = (bf16[2,4,2,32,512]{4,3,2,1,0:T(8,128)(2,1)S(1)}, bf16[2,4,2,32,512]{4,3,2,1,0:T(8,128)(2,1)S(1)}, u32[]{:S(2)}, u32[]{:S(2)}) collective-permute-start(bf16[2,4,2,32,512]{4,3,2,1,0:T(8,128)(2,1)S(1)} %bitcast.52), channel_id=1, source_target_pairs={{4,0},{65,1},{8,4},{69,5},{12,8},{73,9},{16,12},{77,13},{20,16},{8... | collective-permute-start | bytes 1572872 | tf_op jit(solution)/shard_map/ppermute | solution.py:40
  59.0 18.1 %collective-permute-start.7 = (bf16[2,4,2,32,512]{4,3,2,1,0:T(8,128)(2,1)S(1)}, bf16[2,4,2,32,512]{4,3,2,1,0:T(8,128)(2,1)S(1)}, u32[]{:S(2)}, u32[]{:S(2)}) collective-permute-start(bf16[2,4,2,32,512]{4,3,2,1,0:T(8,128)(2,1)S(1)} %bitcast.53), channel_id=1, source_target_pairs={{60,0},{193,1},{0,4},{197,5},{4,8},{201,9},{8,12},{205,13},{12,16}... | collective-permute-start | bytes 1572872 | tf_op jit(solution)/shard_map/ppermute | solution.py:40
  61.0 15.9 %collective-permute-start.5 = (bf16[1,4,2,32,512]{4,3,2,1,0:T(8,128)(2,1)S(1)}, bf16[1,4,2,32,512]{4,3,2,1,0:T(8,128)(2,1)S(1)}, u32[]{:S(2)}, u32[]{:S(2)}) collective-permute-start(bf16[1,4,2,32,512]{4,3,2,1,0:T(8,128)(2,1)S(1)} %get-tuple-element.38), channel_id=1, source_target_pairs={{8,0},{129,1},{12,4},{133,5},{16,8},{137,9},{20,12},{141,13},{24,1... | collective-permute-start | bytes 786440 | tf_op jit(solution)/shard_map/ppermute | solution.py:40
  64.7 12.3 %collective-permute-start.6 = (bf16[1,4,2,32,512]{4,3,2,1,0:T(8,128)(2,1)S(1)}, bf16[1,4,2,32,512]{4,3,2,1,0:T(8,128)(2,1)S(1)}, u32[]{:S(2)}, u32[]{:S(2)}) collective-permute-start(bf16[1,4,2,32,512]{4,3,2,1,0:T(8,128)(2,1)S(1)} %get-tuple-element.37), channel_id=1, source_target_pairs={{56,0},{129,1},{60,4},{133,5},{0,8},{137,9},{4,12},{141,13},{8,16}... | collective-permute-start | bytes 786440 | tf_op jit(solution)/shard_map/ppermute | solution.py:40
  71.2 32.7 %collective-permute-start.2 = (bf16[2,256,2048]{2,1,0:T(8,128)(2,1)}, bf16[2,256,2048]{2,1,0:T(8,128)(2,1)}, u32[]{:S(2)}, u32[]{:S(2)}) collective-permute-start(bf16[2,256,2048]{2,1,0:T(8,128)(2,1)} %pad_maximum_fusion.1), channel_id=1, source_target_pairs={{0,1},{1,0},{2,3},{3,2},{4,5},{5,4},{6,7},{7,6},{8,9},{9,8},{10,11... | collective-permute-start | bytes 6291464 | tf_op jit(solution)/shard_map/ppermute | solution.py:26
  78.5 18.8 %collective-permute-start.13 = (bf16[4,2,4,2,32,256]{5,4,3,2,1,0:T(8,128)(2,1)}, bf16[4,2,4,2,32,256]{5,4,3,2,1,0:T(8,128)(2,1)}, u32[]{:S(2)}, u32[]{:S(2)}) collective-permute-start(bf16[4,2,4,2,32,256]{5,4,3,2,1,0:T(8,128)(2,1)} %get-tuple-element.13.refs_0_), channel_id=1, source_target_pairs={{192,0},{61,1},{196,4},{1,5},{200,8},{5,9},{204,12},{9,13},{208,16... | collective-permute-start | bytes 3145736 | tf_op jit(solution)/shard_map/ppermute | solution.py:40
  81.9 17.4 %collective-permute-start.8 = (bf16[4,2,4,2,32,256]{5,4,3,2,1,0:T(8,128)(2,1)S(1)}, bf16[4,2,4,2,32,256]{5,4,3,2,1,0:T(8,128)(2,1)}, u32[]{:S(2)}, u32[]{:S(2)}) collective-permute-start(bf16[4,2,4,2,32,256]{5,4,3,2,1,0:T(8,128)(2,1)S(1)} %get-tuple-element.12.refs_0_), channel_id=1, source_target_pairs={{64,0},{5,1},{68,4},{9,5},{72,8},{13,9},{76,12},{17,13},{80,16},{2... | collective-permute-start | bytes 3145736 | tf_op jit(solution)/shard_map/ppermute | solution.py:40
  86.5 52.5 %copy-start.6 = (s32[3]{0:T(128)}, s32[3]{0:T(128)S(1)}, u32[]{:S(2)}) copy-start(s32[3]{0:T(128)S(1)} %pad_add_fusion.place) | copy-start | bytes 40
  86.5 23.0 %collective-permute-start.12 = (bf16[4,2,4,2,32,256]{5,4,3,2,1,0:T(8,128)(2,1)}, bf16[4,2,4,2,32,256]{5,4,3,2,1,0:T(8,128)(2,1)S(1)}, u32[]{:S(2)}, u32[]{:S(2)}) collective-permute-start(bf16[4,2,4,2,32,256]{5,4,3,2,1,0:T(8,128)(2,1)} %get-tuple-element.13.refs_0_), channel_id=1, source_target_pairs={{64,0},{5,1},{68,4},{9,5},{72,8},{13,9},{76,12},{17,13},{80,16},{2... | collective-permute-start | bytes 3145736 | tf_op jit(solution)/shard_map/ppermute | solution.py:40
  89.9 41.4 %collective-permute-start.10 = (bf16[4,2,4,2,32,256]{5,4,3,2,1,0:T(8,128)(2,1)S(1)}, bf16[4,2,4,2,32,256]{5,4,3,2,1,0:T(8,128)(2,1)S(1)}, u32[]{:S(2)}, u32[]{:S(2)}) collective-permute-start(bf16[4,2,4,2,32,256]{5,4,3,2,1,0:T(8,128)(2,1)S(1)} %get-tuple-element.12.refs_0_), channel_id=1, source_target_pairs={{192,0},{61,1},{196,4},{1,5},{200,8},{5,9},{204,12},{9,13},{208,16... | collective-permute-start | bytes 3145736 | tf_op jit(solution)/shard_map/ppermute | solution.py:40
  97.3 22.4 %collective-permute-start.14 = (bf16[4,2,4,2,32,256]{5,4,3,2,1,0:T(8,128)(2,1)}, bf16[4,2,4,2,32,256]{5,4,3,2,1,0:T(8,128)(2,1)S(1)}, u32[]{:S(2)}, u32[]{:S(2)}) collective-permute-start(bf16[4,2,4,2,32,256]{5,4,3,2,1,0:T(8,128)(2,1)} %collective-permute-done.13.refs_3_), channel_id=1, source_target_pairs={{192,0},{61,1},{196,4},{1,5},{200,8},{5,9},{204,12},{9,13},{208,16... | collective-permute-start | bytes 3145736 | tf_op jit(solution)/shard_map/ppermute | solution.py:40
  99.2 32.1 %collective-permute-start.9 = (bf16[4,2,4,2,32,256]{5,4,3,2,1,0:T(8,128)(2,1)}, bf16[4,2,4,2,32,256]{5,4,3,2,1,0:T(8,128)(2,1)S(1)}, u32[]{:S(2)}, u32[]{:S(2)}) collective-permute-start(bf16[4,2,4,2,32,256]{5,4,3,2,1,0:T(8,128)(2,1)} %collective-permute-done.8.refs_1_), channel_id=1, source_target_pairs={{64,0},{5,1},{68,4},{9,5},{72,8},{13,9},{76,12},{17,13},{80,16},{2... | collective-permute-start | bytes 3145736 | tf_op jit(solution)/shard_map/ppermute | solution.py:40
  106.6 24.7 %copy-start = (bf16[4,128,2048]{2,1,0:T(8,128)(2,1)}, bf16[4,128,2048]{2,1,0:T(8,128)(2,1)S(1)}, u32[]{:S(2)}) copy-start(bf16[4,128,2048]{2,1,0:T(8,128)(2,1)S(1)} %get-tuple-element.21) | copy-start | bytes 6291460
  127.9 11.2 %collective-permute-start.15 = (bf16[3,512,256]{2,1,0:T(8,128)(2,1)}, bf16[3,512,256]{2,1,0:T(8,128)(2,1)}, u32[]{:S(2)}, u32[]{:S(2)}) collective-permute-start(bf16[3,512,256]{2,1,0:T(8,128)(2,1)} %get-tuple-element.14), channel_id=1, source_target_pairs={{0,1},{1,0},{2,3},{3,2},{4,5},{5,4},{6,7},{7,6},{8,9},{9,8},{10,11... | collective-permute-start | bytes 2359304 | tf_op jit(solution)/shard_map/ppermute | solution.py:26
  131.3 5.1 %copy-start.2 = (bf16[4,2,4,2,32,256]{5,4,3,2,1,0:T(8,128)(2,1)}, bf16[4,2,4,2,32,256]{5,4,3,2,1,0:T(8,128)(2,1)S(1)}, u32[]{:S(2)}) copy-start(bf16[4,2,4,2,32,256]{5,4,3,2,1,0:T(8,128)(2,1)S(1)} %collective-permute-done.10.refs_3_) | copy-start | bytes 3145732
  131.3 5.1 %copy-start.4 = (bf16[4,2,4,2,32,256]{5,4,3,2,1,0:T(8,128)(2,1)}, bf16[4,2,4,2,32,256]{5,4,3,2,1,0:T(8,128)(2,1)S(1)}, u32[]{:S(2)}) copy-start(bf16[4,2,4,2,32,256]{5,4,3,2,1,0:T(8,128)(2,1)S(1)} %collective-permute-done.9.refs_2_) | copy-start | bytes 3145732
  136.4 12.2 %collective-permute-start.11 = (bf16[3,512,256]{2,1,0:T(8,128)(2,1)}, bf16[3,512,256]{2,1,0:T(8,128)(2,1)}, u32[]{:S(2)}, u32[]{:S(2)}) collective-permute-start(bf16[3,512,256]{2,1,0:T(8,128)(2,1)} %shard_map.67), channel_id=1, source_target_pairs={{0,1},{1,0},{2,3},{3,2},{4,5},{5,4},{6,7},{7,6},{8,9},{9,8},{10,11... | collective-permute-start | bytes 2359304 | tf_op jit(solution)/shard_map/ppermute | solution.py:26
  (3 other events, 4.0 us)

commit v3 on v2

--- a/solution.py
+++ b/solution.py
@@ -46,17 +46,19 @@
     return jnp.concatenate([first, second], dim)
 
 
-def near_weight(proj_old):
+def near_weight(proj_old, outgoing):
     c = lax.axis_index("c")
     half = proj_old.shape[1] // 2
     mine = lax.dynamic_slice_in_dim(proj_old, c * half, half, 1)
     given = lax.dynamic_slice_in_dim(proj_old, (1 - c) * half, half, 1)
     taken = swap(given, "c")
     mates = lax.all_gather(jnp.stack([mine, taken]), "u")
+    mates, outgoing = lax.optimization_barrier((mates, outgoing))
+    incoming = swap_parity(outgoing)
     planes = lax.all_gather(mates, "y")
     after, before = along(planes, 1, 1), along(planes, 1, -1)
     opposite = [along(planes[:1], 1, 2), along(planes[1:], 1, -2)]
-    return [planes, after, jnp.concatenate(opposite, 0), before]
+    return [planes, after, jnp.concatenate(opposite, 0), before], incoming
 
 
 def all_weight(pieces):
@@ -72,20 +74,26 @@
     return (low, low_after, low_far, low_before), (high, high_after, high_far, high_before)
 
 
-def pair_exchange(vlm_tokens, action_tokens, norm_gain, proj_old):
-    b = lax.axis_index("w") % 2
+def for_neighbour(vlm_tokens, norm_gain, proj_old):
     row_half, width = proj_old.shape[0] // 2, vlm_tokens.shape[1]
     vlm = normalize(vlm_tokens, norm_gain)
+    b = lax.axis_index("w") % 2
+    given = lax.dynamic_slice_in_dim(proj_old, (1 - b) * row_half, row_half, 0)
+    given = jnp.concatenate(jnp.split(given, width // given.shape[1], 0), 1)
+    return jnp.concatenate([vlm, given], 0)
+
+
+def with_neighbour(outgoing, incoming, action_tokens, norm_gain, proj_old):
+    b = lax.axis_index("w") % 2
+    row_half, width = proj_old.shape[0] // 2, outgoing.shape[1]
+    folds = width // proj_old.shape[1]
+    count = outgoing.shape[0] - row_half // folds
     action = normalize(action_tokens, norm_gain)
+    tokens = jnp.concatenate([both(b, outgoing[:count], incoming[:count], 0), action], 0)
     kept = lax.dynamic_slice_in_dim(proj_old, b * row_half, row_half, 0)
-    given = lax.dynamic_slice_in_dim(proj_old, (1 - b) * row_half, row_half, 0)
-    folds = width // given.shape[1]
-    given = jnp.concatenate(jnp.split(given, folds, 0), 1)
-    other = swap_parity(jnp.concatenate([vlm, given], 0))
-    pair = both(b, vlm, other[: vlm.shape[0]], 0)
-    taken = jnp.concatenate(jnp.split(other[vlm.shape[0] :], folds, 1), 0)
+    taken = jnp.concatenate(jnp.split(incoming[count:], folds, 1), 0)
     rows = both(b, kept, taken, 1)
-    return jnp.concatenate([pair, action], 0), rows
+    return tokens, rows
 
 
 def all_tokens(mine, n_vlm):
@@ -240,8 +248,9 @@
 
 
 def local(vlm_tokens, action_tokens, norm_gain, proj_old):
-    pieces = near_weight(proj_old)
-    mine, proj_new = pair_exchange(vlm_tokens, action_tokens, norm_gain, proj_old)
+    outgoing = for_neighbour(vlm_tokens, norm_gain, proj_old)
+    pieces, incoming = near_weight(proj_old, outgoing)
+    mine, proj_new = with_neighbour(outgoing, incoming, action_tokens, norm_gain, proj_old)
     slabs = all_weight(pieces)
     vlm, action = all_tokens(mine, vlm_tokens.shape[0])
     vlm_hidden, action_hidden = outputs(vlm, action, slabs)

time: 153 us -> 171 us (1.12)
  blocking collectives: 30.4 us -> 44.2 us
  waiting for transfers between devices: 21.1 us -> 23.1 us
    all_gather x1, blocking collectives: 5.87 us -> 25 us  [near_weight(): planes = lax.all_gather(mates, 'y')]
    all_gather x1, blocking collectives: 24.5 us -> 19.2 us  [near_weight(): mates = lax.all_gather(jnp.stack([mine, taken]), 'u')]
    ppermute x5, starting transfers between devices: 22 us -> 25.7 us  [swap(): return lax.ppermute(array, axis, [(0, 1), (1, 0)])]
    ppermute x1, waiting for transfers between devices: 1.91 us -> 4.68 us  [swap_parity(): return lax.ppermute(array, 'w', [(i, i ^ 1) for i in range(NW)])]
    ppermute x1, starting transfers between devices: 4.36 us -> 2.56 us  [swap_parity(): return lax.ppermute(array, 'w', [(i, i ^ 1) for i in range(NW)])]
  transfers between devices with their start and end apart: 16 -> 16, of which waited for: 5 -> 4; matrix products, arithmetic and copies ran while one was open for 7% -> 8% of each run, Pallas kernels for 12% -> 11%
where the time goes in v3:
time: 171 us; the launch traced here: 168 us
  starting transfers between devices  60.6 us (35%)
  blocking collectives  44.2 us (26%)
  waiting for transfers between devices  23.1 us (14%)
  Pallas kernels  20.8 us (12%)
  other arithmetic  11.4 us (7%)
  local copies, waits for them, and re-layouts  6.66 us (4%)
    ppermute x10, starting transfers between devices, along(): return lax.ppermute(array, PLANE, pairs)  32.3 us
    ppermute x5, starting transfers between devices, swap(): return lax.ppermute(array, axis, [(0, 1), (1, 0)])  25.7 us
    all_gather x1, blocking collectives, near_weight(): planes = lax.all_gather(mates, 'y')  25 us
    all_gather x1, blocking collectives, near_weight(): mates = lax.all_gather(jnp.stack([mine, taken]), 'u')  19.2 us
    pallas_call x3, Pallas kernels, call(): pl.pallas_call(kernel, out_shape=(taken,) * given + wide * own, in_specs=...  18.8 us
    ppermute x10, waiting for transfers between devices, along(): return lax.ppermute(array, PLANE, pairs)  18.4 us
    ppermute x1, waiting for transfers between devices, swap_parity(): return lax.ppermute(array, 'w', [(i, i ^ 1) for i in range(NW)])  4.68 us
    unnamed x23, local copies, waits for them, and re-layouts  4.1 us
  transfers between devices with their start and end apart: 16, of which 4 were waited for; matrix products, arithmetic and copies ran while one was open for 8% of the time, Pallas kernels for 11%

profile of v3, /device:TPU:1, one launch (start us, length us, event | category | flops | bytes accessed | tf_op | source)
XLA Modules:
  0.0 168.0 jit_solution(6715081824661303312)
XLA Ops:
  1.5 8.7 %collective-permute-start = (bf16[32,512]{1,0:T(8,128)(2,1)S(1)}, bf16[32,512]{1,0:T(8,128)(2,1)S(1)}, u32[]{:S(2)}, u32[]{:S(2)}) collective-permute-start(bf16[32,512]{1,0:T(8,128)(2,1)S(1)} %get-tuple-element.50), channel_id=1, source_target_pairs={{0,1},{1,0},{2,3},{3,2},{4,5},{5,4},{6,7},{7,6},{8,9},{9,8},{10,11... | collective-permute-start | bytes 98312 | tf_op jit(solution)/shard_map/ppermute | solution.py:26
  14.5 19.2 %all-gather = bf16[8,32,512]{2,1,0:T(8,128)(2,1)S(1)} all-gather(bf16[2,32,512]{2,1,0:T(8,128)(2,1)S(1)} %pad_maximum_fusion.5), channel_id=2, replica_groups=mesh['y'=2,'x'=4,'u'=4,'w'=4,'h'=2,'c'=2] {'u'}, dimensions={0}, use_global_device_ids=true | all-gather | bytes 327680 | tf_op jit(solution)/shard_map/all_gather | solution.py:55
  33.7 2.6 %collective-permute-start.1 = (bf16[72,2048]{1,0:T(8,128)(2,1)S(1)}, bf16[72,2048]{1,0:T(8,128)(2,1)S(1)}, u32[]{:S(2)}, u32[]{:S(2)}) collective-permute-start(bf16[72,2048]{1,0:T(8,128)(2,1)S(1)} %maximum_maximum_fusion), channel_id=1, source_target_pairs={{0,4},{4,0},{8,12},{12,8},{1,5},{5,1},{9,13},{13,9},{2,6},{6,2},{1... | collective-permute-start | bytes 884744 | tf_op jit(solution)/shard_map/ppermute | solution.py:30
  36.5 4.7 %collective-permute-done.1 = bf16[72,2048]{1,0:T(8,128)(2,1)S(1)} collective-permute-done((bf16[72,2048]{1,0:T(8,128)(2,1)S(1)}, bf16[72,2048]{1,0:T(8,128)(2,1)S(1)}, u32[]{:S(2)}, u32[]{:S(2)}) %collective-permute-start.1) | collective-permute-done | bytes 294944 | tf_op jit(solution)/shard_map/ppermute | solution.py:30
  41.5 4.8 %collective-permute-start.2 = (bf16[256,2048]{1,0:T(8,128)(2,1)S(1)}, bf16[256,2048]{1,0:T(8,128)(2,1)}, u32[]{:S(2)}, u32[]{:S(2)}) collective-permute-start(bf16[256,2048]{1,0:T(8,128)(2,1)S(1)} %pad_maximum_fusion.2), channel_id=1, source_target_pairs={{0,2},{2,0},{1,3},{3,1},{4,6},{6,4},{5,7},{7,5},{8,10},{10,8},{9,1... | collective-permute-start | bytes 3145736 | tf_op jit(solution)/shard_map/ppermute | solution.py:26
  46.3 25.0 %all-gather.1 = bf16[8,2,32,512]{3,2,1,0:T(8,128)(2,1)S(1)} all-gather(bf16[4,2,32,512]{3,2,1,0:T(8,128)(2,1)S(1)} %bitcast.55), channel_id=3, replica_groups=mesh['y'=2,'x'=4,'u'=4,'w'=4,'h'=2,'c'=2] {'y'}, dimensions={0}, use_global_device_ids=true | all-gather | bytes 786432 | tf_op jit(solution)/shard_map/all_gather | solution.py:58
  71.4 4.4 %collective-permute-start.4 = (bf16[2,4,2,32,512]{4,3,2,1,0:T(8,128)(2,1)S(1)}, bf16[2,4,2,32,512]{4,3,2,1,0:T(8,128)(2,1)S(1)}, u32[]{:S(2)}, u32[]{:S(2)}) collective-permute-start(bf16[2,4,2,32,512]{4,3,2,1,0:T(8,128)(2,1)S(1)} %bitcast.52), channel_id=1, source_target_pairs={{4,0},{65,1},{8,4},{69,5},{12,8},{73,9},{16,12},{77,13},{20,16},{8... | collective-permute-start | bytes 1572872 | tf_op jit(solution)/shard_map/ppermute | solution.py:40
  75.7 1.9 %collective-permute-start.7 = (bf16[2,4,2,32,512]{4,3,2,1,0:T(8,128)(2,1)S(1)}, bf16[2,4,2,32,512]{4,3,2,1,0:T(8,128)(2,1)S(1)}, u32[]{:S(2)}, u32[]{:S(2)}) collective-permute-start(bf16[2,4,2,32,512]{4,3,2,1,0:T(8,128)(2,1)S(1)} %bitcast.53), channel_id=1, source_target_pairs={{60,0},{193,1},{0,4},{197,5},{4,8},{201,9},{8,12},{205,13},{12,16}... | collective-permute-start | bytes 1572872 | tf_op jit(solution)/shard_map/ppermute | solution.py:40
  77.7 3.6 %collective-permute-start.5 = (bf16[1,4,2,32,512]{4,3,2,1,0:T(8,128)(2,1)S(1)}, bf16[1,4,2,32,512]{4,3,2,1,0:T(8,128)(2,1)S(1)}, u32[]{:S(2)}, u32[]{:S(2)}) collective-permute-start(bf16[1,4,2,32,512]{4,3,2,1,0:T(8,128)(2,1)S(1)} %get-tuple-element.42), channel_id=1, source_target_pairs={{8,0},{129,1},{12,4},{133,5},{16,8},{137,9},{20,12},{141,13},{24,1... | collective-permute-start | bytes 786440 | tf_op jit(solution)/shard_map/ppermute | solution.py:40
  81.4 3.2 %collective-permute-start.6 = (bf16[1,4,2,32,512]{4,3,2,1,0:T(8,128)(2,1)S(1)}, bf16[1,4,2,32,512]{4,3,2,1,0:T(8,128)(2,1)S(1)}, u32[]{:S(2)}, u32[]{:S(2)}) collective-permute-start(bf16[1,4,2,32,512]{4,3,2,1,0:T(8,128)(2,1)S(1)} %get-tuple-element.41), channel_id=1, source_target_pairs={{56,0},{129,1},{60,4},{133,5},{0,8},{137,9},{4,12},{141,13},{8,16}... | collective-permute-start | bytes 786440 | tf_op jit(solution)/shard_map/ppermute | solution.py:40
  87.9 6.4 %collective-permute-start.3 = (bf16[2,256,2048]{2,1,0:T(8,128)(2,1)}, bf16[2,256,2048]{2,1,0:T(8,128)(2,1)}, u32[]{:S(2)}, u32[]{:S(2)}) collective-permute-start(bf16[2,256,2048]{2,1,0:T(8,128)(2,1)} %pad_maximum_fusion.1), channel_id=1, source_target_pairs={{0,1},{1,0},{2,3},{3,2},{4,5},{5,4},{6,7},{7,6},{8,9},{9,8},{10,11... | collective-permute-start | bytes 6291464 | tf_op jit(solution)/shard_map/ppermute | solution.py:26
  95.8 2.9 %collective-permute-start.13 = (bf16[4,2,4,2,32,256]{5,4,3,2,1,0:T(8,128)(2,1)}, bf16[4,2,4,2,32,256]{5,4,3,2,1,0:T(8,128)(2,1)}, u32[]{:S(2)}, u32[]{:S(2)}) collective-permute-start(bf16[4,2,4,2,32,256]{5,4,3,2,1,0:T(8,128)(2,1)} %get-tuple-element.17.refs_0_), channel_id=1, source_target_pairs={{192,0},{61,1},{196,4},{1,5},{200,8},{5,9},{204,12},{9,13},{208,16... | collective-permute-start | bytes 3145736 | tf_op jit(solution)/shard_map/ppermute | solution.py:40
  98.7 4.6 %collective-permute-start.8 = (bf16[4,2,4,2,32,256]{5,4,3,2,1,0:T(8,128)(2,1)S(1)}, bf16[4,2,4,2,32,256]{5,4,3,2,1,0:T(8,128)(2,1)}, u32[]{:S(2)}, u32[]{:S(2)}) collective-permute-start(bf16[4,2,4,2,32,256]{5,4,3,2,1,0:T(8,128)(2,1)S(1)} %get-tuple-element.16.refs_0_), channel_id=1, source_target_pairs={{64,0},{5,1},{68,4},{9,5},{72,8},{13,9},{76,12},{17,13},{80,16},{2... | collective-permute-start | bytes 3145736 | tf_op jit(solution)/shard_map/ppermute | solution.py:40
  103.4 3.4 %collective-permute-start.12 = (bf16[4,2,4,2,32,256]{5,4,3,2,1,0:T(8,128)(2,1)}, bf16[4,2,4,2,32,256]{5,4,3,2,1,0:T(8,128)(2,1)S(1)}, u32[]{:S(2)}, u32[]{:S(2)}) collective-permute-start(bf16[4,2,4,2,32,256]{5,4,3,2,1,0:T(8,128)(2,1)} %get-tuple-element.17.refs_0_), channel_id=1, source_target_pairs={{64,0},{5,1},{68,4},{9,5},{72,8},{13,9},{76,12},{17,13},{80,16},{2... | collective-permute-start | bytes 3145736 | tf_op jit(solution)/shard_map/ppermute | solution.py:40
  108.7 5.5 %collective-permute-done.13.refs_3_ = bf16[4,2,4,2,32,256]{5,4,3,2,1,0:T(8,128)(2,1)} collective-permute-done((bf16[4,2,4,2,32,256]{5,4,3,2,1,0:T(8,128)(2,1)}, bf16[4,2,4,2,32,256]{5,4,3,2,1,0:T(8,128)(2,1)}, u32[]{:S(2)}, u32[]{:S(2)}) %collective-permute-start.13) | collective-permute-done | bytes 1048608 | tf_op jit(solution)/shard_map/ppermute | solution.py:40
  116.1 4.6 %collective-permute-start.9 = (bf16[4,2,4,2,32,256]{5,4,3,2,1,0:T(8,128)(2,1)}, bf16[4,2,4,2,32,256]{5,4,3,2,1,0:T(8,128)(2,1)S(1)}, u32[]{:S(2)}, u32[]{:S(2)}) collective-permute-start(bf16[4,2,4,2,32,256]{5,4,3,2,1,0:T(8,128)(2,1)} %collective-permute-done.8.refs_1_), channel_id=1, source_target_pairs={{64,0},{5,1},{68,4},{9,5},{72,8},{13,9},{76,12},{17,13},{80,16},{2... | collective-permute-start | bytes 3145736 | tf_op jit(solution)/shard_map/ppermute | solution.py:40
  123.7 2.7 %collective-permute-done.12.refs_1_ = bf16[4,2,4,2,32,256]{5,4,3,2,1,0:T(8,128)(2,1)S(1)} collective-permute-done((bf16[4,2,4,2,32,256]{5,4,3,2,1,0:T(8,128)(2,1)}, bf16[4,2,4,2,32,256]{5,4,3,2,1,0:T(8,128)(2,1)S(1)}, u32[]{:S(2)}, u32[]{:S(2)}) %collective-permute-start.12) | collective-permute-done | bytes 1048608 | tf_op jit(solution)/shard_map/ppermute | solution.py:40
  126.4 10.2 %collective-permute-done.14.refs_2_ = bf16[4,2,4,2,32,256]{5,4,3,2,1,0:T(8,128)(2,1)S(1)} collective-permute-done((bf16[4,2,4,2,32,256]{5,4,3,2,1,0:T(8,128)(2,1)}, bf16[4,2,4,2,32,256]{5,4,3,2,1,0:T(8,128)(2,1)S(1)}, u32[]{:S(2)}, u32[]{:S(2)}) %collective-permute-start.14) | collective-permute-done | bytes 1048608 | tf_op jit(solution)/shard_map/ppermute | solution.py:40
  136.5 8.2 %shard_map.68 = (bf16[3,512,256]{2,1,0:T(8,128)(2,1)}, bf16[512,1024]{1,0:T(8,128)(2,1)}, bf16[512,2048]{1,0:T(8,128)(2,1)}) custom-call(s32[3]{0:T(128)S(1)} %pad_add_fusion.place, bf16[512,2048]{1,0:T(8,128)(2,1)S(1)} %bitcast.44, bf16[512,2048]{1,0:T(8,128)(2,1)S(1)} %bitcast.47, bf16[4,2,4,2,32,256]{5,4,3,2,1,0:T(8,128)(2,1)} %get-tuple-element.17.refs_0_, ...), custom_call_target="tpu_custom_call" | custom-call | flops 3221225472 | bytes 6291456 | tf_op jit(solution)/shard_map/pallas_call | solution.py:216
  144.8 3.8 %collective-permute-start.15 = (bf16[3,512,256]{2,1,0:T(8,128)(2,1)}, bf16[3,512,256]{2,1,0:T(8,128)(2,1)}, u32[]{:S(2)}, u32[]{:S(2)}) collective-permute-start(bf16[3,512,256]{2,1,0:T(8,128)(2,1)} %get-tuple-element.18), channel_id=1, source_target_pairs={{0,1},{1,0},{2,3},{3,2},{4,5},{5,4},{6,7},{7,6},{8,9},{9,8},{10,11... | collective-permute-start | bytes 2359304 | tf_op jit(solution)/shard_map/ppermute | solution.py:26
  148.6 5.1 %shard_map.67 = bf16[3,512,256]{2,1,0:T(8,128)(2,1)} custom-call(s32[3]{0:T(128)S(1)} %pad_add_fusion.place, bf16[512,2048]{1,0:T(8,128)(2,1)S(1)} %bitcast.45, bf16[512,2048]{1,0:T(8,128)(2,1)S(1)} %bitcast.48, bf16[4,2,4,2,32,256]{5,4,3,2,1,0:T(8,128)(2,1)S(1)} %get-tuple-element.16.refs_0_, ...), custom_call_target="tpu_custom_call" | custom-call | flops 1610612736 | bytes 6291456 | tf_op jit(solution)/shard_map/pallas_call | solution.py:216
  153.7 1.9 %collective-permute-start.11 = (bf16[3,512,256]{2,1,0:T(8,128)(2,1)}, bf16[3,512,256]{2,1,0:T(8,128)(2,1)}, u32[]{:S(2)}, u32[]{:S(2)}) collective-permute-start(bf16[3,512,256]{2,1,0:T(8,128)(2,1)} %shard_map.67), channel_id=1, source_target_pairs={{0,1},{1,0},{2,3},{3,2},{4,5},{5,4},{6,7},{7,6},{8,9},{9,8},{10,11... | collective-permute-start | bytes 2359304 | tf_op jit(solution)/shard_map/ppermute | solution.py:26
  160.4 5.5 %shard_map.69 = (bf16[512,1024]{1,0:T(8,128)(2,1)}, bf16[512,2048]{1,0:T(8,128)(2,1)}) custom-call(s32[3]{0:T(128)S(1)} %pad_add_fusion.place, bf16[512,2048]{1,0:T(8,128)(2,1)S(1)} %bitcast.46, bf16[512,2048]{1,0:T(8,128)(2,1)S(1)} %bitcast.49, ...), custom_call_target="tpu_custom_call", output_to_operand_aliasing={{0}: (8, {}), {1}: (9, {})} | custom-call | flops 1610612736 | bytes 6291456 | tf_op jit(solution)/shard_map/pallas_call | solution.py:216
  165.9 2.1 %merge.1 = (bf16[512,1024]{1,0:T(8,128)(2,1)}, bf16[512,2048]{1,0:T(8,128)(2,1)}) custom-call(s32[3]{0:T(128)} %copy-done.6, bf16[3,512,256]{2,1,0:T(8,128)(2,1)} %collective-permute-done.11.parts, bf16[512,1024]{1,0:T(8,128)(2,1)} %get-tuple-element.21.vlm_in, ...), custom_call_target="tpu_custom_call", output_to_operand_aliasing={{0}: (2, {}), {1}: (3, {})} | custom-call | tf_op jit(solution)/shard_map/merge/pallas_call | solution.py:239
  (66 shorter events, 22.0 us)
Async XLA Ops:
  0.6 40.5 %copy-start.7 = (bf16[64,2048]{1,0:T(8,128)(2,1)S(1)}, bf16[64,2048]{1,0:T(8,128)(2,1)}, u32[]{:S(2)}) copy-start(bf16[64,2048]{1,0:T(8,128)(2,1)} %param.4) | copy-start | bytes 786436
  0.6 35.6 %copy-start.8 = (bf16[128,2048]{1,0:T(8,128)(2,1)S(1)}, bf16[128,2048]{1,0:T(8,128)(2,1)}, u32[]{:S(2)}) copy-start(bf16[128,2048]{1,0:T(8,128)(2,1)} %param.5) | copy-start | bytes 1572868
  0.7 35.6 %copy-start.10 = (f32[2048]{0:T(1024)S(1)}, f32[2048]{0:T(1024)}, u32[]{:S(2)}) copy-start(f32[2048]{0:T(1024)} %param.6) | copy-start | bytes 24580
  1.5 13.0 %collective-permute-start = (bf16[32,512]{1,0:T(8,128)(2,1)S(1)}, bf16[32,512]{1,0:T(8,128)(2,1)S(1)}, u32[]{:S(2)}, u32[]{:S(2)}) collective-permute-start(bf16[32,512]{1,0:T(8,128)(2,1)S(1)} %get-tuple-element.50), channel_id=1, source_target_pairs={{0,1},{1,0},{2,3},{3,2},{4,5},{5,4},{6,7},{7,6},{8,9},{9,8},{10,11... | collective-permute-start | bytes 98312 | tf_op jit(solution)/shard_map/ppermute | solution.py:26
  33.7 7.5 %collective-permute-start.1 = (bf16[72,2048]{1,0:T(8,128)(2,1)S(1)}, bf16[72,2048]{1,0:T(8,128)(2,1)S(1)}, u32[]{:S(2)}, u32[]{:S(2)}) collective-permute-start(bf16[72,2048]{1,0:T(8,128)(2,1)S(1)} %maximum_maximum_fusion), channel_id=1, source_target_pairs={{0,4},{4,0},{8,12},{12,8},{1,5},{5,1},{9,13},{13,9},{2,6},{6,2},{1... | collective-permute-start | bytes 884744 | tf_op jit(solution)/shard_map/ppermute | solution.py:30
  41.5 43.1 %collective-permute-start.2 = (bf16[256,2048]{1,0:T(8,128)(2,1)S(1)}, bf16[256,2048]{1,0:T(8,128)(2,1)}, u32[]{:S(2)}, u32[]{:S(2)}) collective-permute-start(bf16[256,2048]{1,0:T(8,128)(2,1)S(1)} %pad_maximum_fusion.2), channel_id=1, source_target_pairs={{0,2},{2,0},{1,3},{3,1},{4,6},{6,4},{5,7},{7,5},{8,10},{10,8},{9,1... | collective-permute-start | bytes 3145736 | tf_op jit(solution)/shard_map/ppermute | solution.py:26
  71.4 23.1 %collective-permute-start.4 = (bf16[2,4,2,32,512]{4,3,2,1,0:T(8,128)(2,1)S(1)}, bf16[2,4,2,32,512]{4,3,2,1,0:T(8,128)(2,1)S(1)}, u32[]{:S(2)}, u32[]{:S(2)}) collective-permute-start(bf16[2,4,2,32,512]{4,3,2,1,0:T(8,128)(2,1)S(1)} %bitcast.52), channel_id=1, source_target_pairs={{4,0},{65,1},{8,4},{69,5},{12,8},{73,9},{16,12},{77,13},{20,16},{8... | collective-permute-start | bytes 1572872 | tf_op jit(solution)/shard_map/ppermute | solution.py:40
  75.7 18.8 %collective-permute-start.7 = (bf16[2,4,2,32,512]{4,3,2,1,0:T(8,128)(2,1)S(1)}, bf16[2,4,2,32,512]{4,3,2,1,0:T(8,128)(2,1)S(1)}, u32[]{:S(2)}, u32[]{:S(2)}) collective-permute-start(bf16[2,4,2,32,512]{4,3,2,1,0:T(8,128)(2,1)S(1)} %bitcast.53), channel_id=1, source_target_pairs={{60,0},{193,1},{0,4},{197,5},{4,8},{201,9},{8,12},{205,13},{12,16}... | collective-permute-start | bytes 1572872 | tf_op jit(solution)/shard_map/ppermute | solution.py:40
  77.7 16.6 %collective-permute-start.5 = (bf16[1,4,2,32,512]{4,3,2,1,0:T(8,128)(2,1)S(1)}, bf16[1,4,2,32,512]{4,3,2,1,0:T(8,128)(2,1)S(1)}, u32[]{:S(2)}, u32[]{:S(2)}) collective-permute-start(bf16[1,4,2,32,512]{4,3,2,1,0:T(8,128)(2,1)S(1)} %get-tuple-element.42), channel_id=1, source_target_pairs={{8,0},{129,1},{12,4},{133,5},{16,8},{137,9},{20,12},{141,13},{24,1... | collective-permute-start | bytes 786440 | tf_op jit(solution)/shard_map/ppermute | solution.py:40
  81.4 13.0 %collective-permute-start.6 = (bf16[1,4,2,32,512]{4,3,2,1,0:T(8,128)(2,1)S(1)}, bf16[1,4,2,32,512]{4,3,2,1,0:T(8,128)(2,1)S(1)}, u32[]{:S(2)}, u32[]{:S(2)}) collective-permute-start(bf16[1,4,2,32,512]{4,3,2,1,0:T(8,128)(2,1)S(1)} %get-tuple-element.41), channel_id=1, source_target_pairs={{56,0},{129,1},{60,4},{133,5},{0,8},{137,9},{4,12},{141,13},{8,16}... | collective-permute-start | bytes 786440 | tf_op jit(solution)/shard_map/ppermute | solution.py:40
  87.9 32.8 %collective-permute-start.3 = (bf16[2,256,2048]{2,1,0:T(8,128)(2,1)}, bf16[2,256,2048]{2,1,0:T(8,128)(2,1)}, u32[]{:S(2)}, u32[]{:S(2)}) collective-permute-start(bf16[2,256,2048]{2,1,0:T(8,128)(2,1)} %pad_maximum_fusion.1), channel_id=1, source_target_pairs={{0,1},{1,0},{2,3},{3,2},{4,5},{5,4},{6,7},{7,6},{8,9},{9,8},{10,11... | collective-permute-start | bytes 6291464 | tf_op jit(solution)/shard_map/ppermute | solution.py:26
  95.8 18.3 %collective-permute-start.13 = (bf16[4,2,4,2,32,256]{5,4,3,2,1,0:T(8,128)(2,1)}, bf16[4,2,4,2,32,256]{5,4,3,2,1,0:T(8,128)(2,1)}, u32[]{:S(2)}, u32[]{:S(2)}) collective-permute-start(bf16[4,2,4,2,32,256]{5,4,3,2,1,0:T(8,128)(2,1)} %get-tuple-element.17.refs_0_), channel_id=1, source_target_pairs={{192,0},{61,1},{196,4},{1,5},{200,8},{5,9},{204,12},{9,13},{208,16... | collective-permute-start | bytes 3145736 | tf_op jit(solution)/shard_map/ppermute | solution.py:40
  98.7 17.4 %collective-permute-start.8 = (bf16[4,2,4,2,32,256]{5,4,3,2,1,0:T(8,128)(2,1)S(1)}, bf16[4,2,4,2,32,256]{5,4,3,2,1,0:T(8,128)(2,1)}, u32[]{:S(2)}, u32[]{:S(2)}) collective-permute-start(bf16[4,2,4,2,32,256]{5,4,3,2,1,0:T(8,128)(2,1)S(1)} %get-tuple-element.16.refs_0_), channel_id=1, source_target_pairs={{64,0},{5,1},{68,4},{9,5},{72,8},{13,9},{76,12},{17,13},{80,16},{2... | collective-permute-start | bytes 3145736 | tf_op jit(solution)/shard_map/ppermute | solution.py:40
  103.4 52.9 %copy-start.6 = (s32[3]{0:T(128)}, s32[3]{0:T(128)S(1)}, u32[]{:S(2)}) copy-start(s32[3]{0:T(128)S(1)} %pad_add_fusion.place) | copy-start | bytes 40
  103.4 23.0 %collective-permute-start.12 = (bf16[4,2,4,2,32,256]{5,4,3,2,1,0:T(8,128)(2,1)}, bf16[4,2,4,2,32,256]{5,4,3,2,1,0:T(8,128)(2,1)S(1)}, u32[]{:S(2)}, u32[]{:S(2)}) collective-permute-start(bf16[4,2,4,2,32,256]{5,4,3,2,1,0:T(8,128)(2,1)} %get-tuple-element.17.refs_0_), channel_id=1, source_target_pairs={{64,0},{5,1},{68,4},{9,5},{72,8},{13,9},{76,12},{17,13},{80,16},{2... | collective-permute-start | bytes 3145736 | tf_op jit(solution)/shard_map/ppermute | solution.py:40
  106.8 41.8 %collective-permute-start.10 = (bf16[4,2,4,2,32,256]{5,4,3,2,1,0:T(8,128)(2,1)S(1)}, bf16[4,2,4,2,32,256]{5,4,3,2,1,0:T(8,128)(2,1)S(1)}, u32[]{:S(2)}, u32[]{:S(2)}) collective-permute-start(bf16[4,2,4,2,32,256]{5,4,3,2,1,0:T(8,128)(2,1)S(1)} %get-tuple-element.16.refs_0_), channel_id=1, source_target_pairs={{192,0},{61,1},{196,4},{1,5},{200,8},{5,9},{204,12},{9,13},{208,16... | collective-permute-start | bytes 3145736 | tf_op jit(solution)/shard_map/ppermute | solution.py:40
  114.2 22.4 %collective-permute-start.14 = (bf16[4,2,4,2,32,256]{5,4,3,2,1,0:T(8,128)(2,1)}, bf16[4,2,4,2,32,256]{5,4,3,2,1,0:T(8,128)(2,1)S(1)}, u32[]{:S(2)}, u32[]{:S(2)}) collective-permute-start(bf16[4,2,4,2,32,256]{5,4,3,2,1,0:T(8,128)(2,1)} %collective-permute-done.13.refs_3_), channel_id=1, source_target_pairs={{192,0},{61,1},{196,4},{1,5},{200,8},{5,9},{204,12},{9,13},{208,16... | collective-permute-start | bytes 3145736 | tf_op jit(solution)/shard_map/ppermute | solution.py:40
  116.1 32.5 %collective-permute-start.9 = (bf16[4,2,4,2,32,256]{5,4,3,2,1,0:T(8,128)(2,1)}, bf16[4,2,4,2,32,256]{5,4,3,2,1,0:T(8,128)(2,1)S(1)}, u32[]{:S(2)}, u32[]{:S(2)}) collective-permute-start(bf16[4,2,4,2,32,256]{5,4,3,2,1,0:T(8,128)(2,1)} %collective-permute-done.8.refs_1_), channel_id=1, source_target_pairs={{64,0},{5,1},{68,4},{9,5},{72,8},{13,9},{76,12},{17,13},{80,16},{2... | collective-permute-start | bytes 3145736 | tf_op jit(solution)/shard_map/ppermute | solution.py:40
  123.5 25.1 %copy-start = (bf16[4,128,2048]{2,1,0:T(8,128)(2,1)}, bf16[4,128,2048]{2,1,0:T(8,128)(2,1)S(1)}, u32[]{:S(2)}) copy-start(bf16[4,128,2048]{2,1,0:T(8,128)(2,1)S(1)} %get-tuple-element.25) | copy-start | bytes 6291460
  144.7 10.9 %copy-start.9 = (bf16[32,1024]{1,0:T(8,128)(2,1)S(1)}, bf16[32,1024]{1,0:T(8,128)(2,1)}, u32[]{:S(2)}) copy-start(bf16[32,1024]{1,0:T(8,128)(2,1)} %param.7) | copy-start | bytes 196612
  144.8 11.6 %collective-permute-start.15 = (bf16[3,512,256]{2,1,0:T(8,128)(2,1)}, bf16[3,512,256]{2,1,0:T(8,128)(2,1)}, u32[]{:S(2)}, u32[]{:S(2)}) collective-permute-start(bf16[3,512,256]{2,1,0:T(8,128)(2,1)} %get-tuple-element.18), channel_id=1, source_target_pairs={{0,1},{1,0},{2,3},{3,2},{4,5},{5,4},{6,7},{7,6},{8,9},{9,8},{10,11... | collective-permute-start | bytes 2359304 | tf_op jit(solution)/shard_map/ppermute | solution.py:26
  148.6 5.1 %copy-start.2 = (bf16[4,2,4,2,32,256]{5,4,3,2,1,0:T(8,128)(2,1)}, bf16[4,2,4,2,32,256]{5,4,3,2,1,0:T(8,128)(2,1)S(1)}, u32[]{:S(2)}) copy-start(bf16[4,2,4,2,32,256]{5,4,3,2,1,0:T(8,128)(2,1)S(1)} %collective-permute-done.10.refs_3_) | copy-start | bytes 3145732
  148.6 5.1 %copy-start.4 = (bf16[4,2,4,2,32,256]{5,4,3,2,1,0:T(8,128)(2,1)}, bf16[4,2,4,2,32,256]{5,4,3,2,1,0:T(8,128)(2,1)S(1)}, u32[]{:S(2)}) copy-start(bf16[4,2,4,2,32,256]{5,4,3,2,1,0:T(8,128)(2,1)S(1)} %collective-permute-done.9.refs_2_) | copy-start | bytes 3145732
  153.7 12.2 %collective-permute-start.11 = (bf16[3,512,256]{2,1,0:T(8,128)(2,1)}, bf16[3,512,256]{2,1,0:T(8,128)(2,1)}, u32[]{:S(2)}, u32[]{:S(2)}) collective-permute-start(bf16[3,512,256]{2,1,0:T(8,128)(2,1)} %shard_map.67), channel_id=1, source_target_pairs={{0,1},{1,0},{2,3},{3,2},{4,5},{5,4},{6,7},{7,6},{8,9},{9,8},{10,11... | collective-permute-start | bytes 2359304 | tf_op jit(solution)/shard_map/ppermute | solution.py:26
  (3 other events, 4.0 us)
